TPU v7x, 32 devices: a whole 2x2x4 slice. The times are simulated.
32 devices in a mesh: seq: 4 (over z), uly: 4 (over y, x), rep: 2 (over core).
Axes of the slice: x: 2, y: 2, z: 4, core: 2. Of those that a mesh axis runs over, the one named last changes fastest.
Arguments:
- queries: bfloat16 [4096, 2048], P(('rep', 'seq', 'uly')), parts along dimension 0, may hold values from -6 to 6
- keys: bfloat16 [4096, 2048], P(('rep', 'seq', 'uly')), parts along dimension 0, may hold values from -6 to 6
- values: bfloat16 [4096, 2048], P(('rep', 'seq', 'uly')), parts along dimension 0, may hold values from -6 to 6
- past_outputs: bfloat16 [2, 4096, 2048], P(None, ('rep', 'seq', 'uly')), parts along dimension 1, may hold values from -6 to 6
- dwa_slot: int32 [2], replicated, may hold values from 0 to 63
- dwa_table: float32 [2, 64], replicated, may hold values from 0.1 to 0.6
Outputs:
- mixed: bfloat16 [4096, 2048], P(('rep', 'seq', 'uly')), parts along dimension 0
There are 2 independent parts, one for each index of `rep`. A program takes and returns all parts, laid end to end along the dimension named above; an argument that names none is the same for every part. Nothing has to cross between parts.
All inputs are finite; a program needn't handle non-finite values.
Results may differ from a plain program's by a relative error of at most 0.0034.
Values may be sent and summed in bfloat16 or wider, within the bound.
A program may use at most 64 MiB of HBM per device.

v0:
```python
import functools
import math

import jax
import jax.numpy as jnp
from jax import lax
from jax.experimental import pallas as pl
from jax.experimental.pallas import tpu as pltpu
from jax.sharding import PartitionSpec as P

HEAD_DIM = 128
SPAN = 4
STAT = 16
MESH = pl.DeviceIdType.MESH
Q, K, V = 0, 1, 2


def from_behind(block, axis, distance):
    devices = range(lax.axis_size(axis))
    route = [(i - distance, i) for i in devices if i - distance in devices]
    return lax.ppermute(block, axis, route)


def block_update(state, query_heads, key_heads, value_heads, allowed):
    running, total, accumulated = state
    scores = jnp.einsum("qhd,khd->hqk", query_heads, key_heads, preferred_element_type=jnp.float32)
    scores = scores * (1.0 / HEAD_DIM**0.5)
    scores = jnp.where(allowed, scores, -jnp.inf)
    new_max = jnp.maximum(running, jnp.max(scores, axis=2))
    factor = jnp.exp(running - new_max)
    prob = jnp.exp(scores - new_max[:, :, None])
    total = total * factor + jnp.sum(prob, axis=2)
    weights = prob.astype(jnp.bfloat16)
    update = jnp.einsum("hqk,khd->qhd", weights, value_heads, preferred_element_type=jnp.float32)
    accumulated = accumulated * jnp.transpose(factor)[:, :, None] + update
    return (new_max, total, accumulated)


def shards(queries, keys, values, past_outputs, dwa_slot, dwa_table):
    n_uly = lax.axis_size("uly")
    n_seq = lax.axis_size("seq")
    span_size = min(4, n_seq)
    features = queries.shape[1]
    local_heads = features // n_uly // HEAD_DIM
    query_rows, key_rows, value_rows = (
        lax.all_to_all(queries, "uly", split_axis=1, concat_axis=0, tiled=True),
        lax.all_to_all(keys, "uly", split_axis=1, concat_axis=0, tiled=True),
        lax.all_to_all(values, "uly", split_axis=1, concat_axis=0, tiled=True),
    )
    row_count = query_rows.shape[0]
    split_shape = (row_count, local_heads, HEAD_DIM)
    query_heads = query_rows.reshape(split_shape)
    table_index = jnp.arange(dwa_table.shape[1])
    onehot = (dwa_slot[:, None] == table_index[None, :]).astype(jnp.float32)
    coefs = jnp.dot(onehot, jnp.transpose(dwa_table), precision=lax.Precision.HIGHEST)
    layer_in = jnp.zeros(queries.shape, jnp.float32)
    extra = jnp.zeros(queries.shape, jnp.float32)
    for index in range(past_outputs.shape[0]):
        stored = past_outputs[index].astype(jnp.float32)
        layer_in = layer_in + coefs[index, 0] * stored
        extra = extra + coefs[index, 1] * stored
    running = jnp.full((local_heads, row_count), -jnp.inf, jnp.float32)
    total = jnp.zeros((local_heads, row_count), jnp.float32)
    accumulated = jnp.zeros(split_shape, jnp.float32)
    state = (running, total, accumulated)
    causal = (jnp.arange(row_count)[:, None] >= jnp.arange(row_count)[None, :])[None, :, :]
    state = block_update(
        state, query_heads, key_rows.reshape(split_shape), value_rows.reshape(split_shape), causal
    )
    position = lax.axis_index("seq")
    current = (key_rows, value_rows)
    for offset in range(1, span_size):
        current = from_behind((current[0], current[1]), "seq", 1)
        far_keys = current[0].reshape(split_shape)
        far_values = current[1].reshape(split_shape)

        def take_block(carry, far_keys=far_keys, far_values=far_values):
            return block_update(carry, query_heads, far_keys, far_values, True)

        def keep_block(carry):
            return carry

        state = lax.cond(position >= offset, take_block, keep_block, state)
    running, total, accumulated = state
    attended = accumulated / jnp.transpose(total)[:, :, None]
    attended = attended.astype(jnp.bfloat16).reshape(row_count, local_heads * HEAD_DIM)
    returned = lax.all_to_all(attended, "uly", split_axis=0, concat_axis=1, tiled=True)
    hidden = layer_in + returned.astype(jnp.float32)
    return (hidden + extra).astype(jnp.bfloat16)


def fused_kernel(
    shape,
    slot_ref, table_ref, q_hbm, k_hbm, v_hbm, past_hbm, out_ref,
    given, past, heads, own, own_stat, part_out, part_in, att, back,
    load_sem, past_sem, plane_sem, line_sem, heads_sem, part_send, part_recv, att_sem, back_sem,
):
    n_seq, n_uly, group = shape
    tokens = given.shape[1]
    rows = n_uly * tokens
    half = rows // 2
    scale = math.log2(math.e) / HEAD_DIM**0.5
    s, t = lax.axis_index("seq"), lax.axis_index("uly")
    alone = group - 1
    shared = group - 1
    guest = 0
    late, visit = group, group + 1

    loads = [
        pltpu.make_async_copy(src, given.at[i], load_sem.at[i]) for i, src in enumerate((q_hbm, k_hbm, v_hbm))
    ]
    for load in loads:
        load.start()
    past_load = pltpu.make_async_copy(past_hbm, past, past_sem)
    past_load.start()

    barrier = pltpu.get_barrier_semaphore()
    for d in range(1, n_uly):
        pl.semaphore_signal(barrier, inc=1, device_id={"uly": lax.rem(t + d, n_uly)}, device_id_type=MESH)
    for d in range(1, n_seq):
        pl.semaphore_signal(barrier, inc=1, device_id={"seq": lax.rem(s + d, n_seq)}, device_id_type=MESH)

    @pl.when(s == 3)
    def _():
        for d in range(1, n_uly):
            pl.semaphore_signal(
                barrier, inc=1, device_id={"seq": 2, "uly": lax.rem(t + d, n_uly)}, device_id_type=MESH
            )

    pl.semaphore_wait(barrier, n_uly + n_seq - 2 + jnp.where(s == 2, n_uly - 1, 0))
    for load in loads:
        load.wait()

    def columns(uly, g):
        return pl.ds(pl.multiple_of((uly * group + g) * HEAD_DIM, HEAD_DIM), HEAD_DIM)

    my_rows = pl.ds(pl.multiple_of(t * tokens, tokens), tokens)

    def plane(kind, g, d):
        peer = lax.rem(t + d, n_uly)
        src = given.at[kind, :, columns(peer, g)]
        dst = heads.at[kind, g, s, my_rows, :]
        if d == 0:
            return pltpu.make_async_copy(src, dst, heads_sem.at[kind, g, s])
        return pltpu.make_async_remote_copy(
            src, dst, plane_sem.at[kind, g, d], heads_sem.at[kind, g, s],
            device_id={"uly": peer}, device_id_type=MESH,
        )

    def scatter(kind, g):
        for d in (*range(1, n_uly), 0):
            plane(kind, g, d).start()

    def arrived(kind, g, block):
        ref = heads.at[kind, g, block]
        pltpu.make_async_copy(ref, ref, heads_sem.at[kind, g, block]).wait()

    def line(kind, g, to, lane=0, block=None):
        block = s if block is None else block
        ref = heads.at[kind, g, block]
        return pltpu.make_async_remote_copy(
            ref, ref, line_sem.at[kind, g, lane], heads_sem.at[kind, g, block],
            device_id={"seq": to}, device_id_type=MESH,
        )

    def partial(g, block, to=None, slot=None):
        slot = g if slot is None else slot
        return pltpu.make_async_remote_copy(
            part_out.at[g, block - n_seq // 2], part_in.at[slot],
            part_send.at[g, block - n_seq // 2], part_recv.at[slot],
            device_id={"seq": block if to is None else to}, device_id_type=MESH,
        )

    def returning(g, lane, block, d):
        peer = lax.rem(t + d, n_uly)
        src = att.at[lane, g, pl.ds(pl.multiple_of(peer * tokens, tokens), tokens), :]
        dst = back.at[:, columns(t, g)]
        if block is None and d == 0:
            return pltpu.make_async_copy(src, dst, back_sem.at[g, t])
        where = {"uly": peer} if block is None else {"seq": block, "uly": peer}
        return pltpu.make_async_remote_copy(
            src, dst, att_sem.at[lane, g, d], back_sem.at[g, t], device_id=where, device_id_type=MESH,
        )

    def give_back(g, lane=0, block=None):
        for d in (*range(1, n_uly), 0):
            returning(g, lane, block, d).start()

    def attend(g, block, full, diagonal, finish, resume=None):
        for a in range(2):
            query = heads[Q, g, block, a * half:(a + 1) * half, :]
            top = total = acc = None
            if resume is not None:
                cut = slice(a * half, (a + 1) * half)
                top, total, acc = own_stat[resume, 0:1, cut], own_stat[resume, 1:2, cut], own[resume, :, cut]
            spans = [(j, rows, False) for j in full] + ([(block, (a + 1) * half, True)] if diagonal else [])
            for j, count, masked in spans:
                key = heads[K, g, j, 0:count, :]
                value = heads[V, g, j, 0:count, :]
                scores = lax.dot_general(key, query, (((1,), (1,)), ((), ())), preferred_element_type=jnp.float32)
                scores = scores * scale
                if masked:
                    key_at = lax.broadcasted_iota(jnp.int32, scores.shape, 0)
                    query_at = lax.broadcasted_iota(jnp.int32, scores.shape, 1) + a * half
                    scores = jnp.where(key_at <= query_at, scores, -jnp.inf)
                peak = jnp.max(scores, axis=0, keepdims=True)
                new_top = peak if top is None else jnp.maximum(top, peak)
                prob = jnp.exp2(scores - new_top)
                sums = jnp.sum(prob, axis=0, keepdims=True)
                update = lax.dot_general(
                    value, prob.astype(jnp.bfloat16), (((0,), (0,)), ((), ())), preferred_element_type=jnp.float32
                )
                if top is None:
                    total, acc = sums, update
                else:
                    factor = jnp.exp2(top - new_top)
                    total = total * factor + sums
                    acc = acc * factor + update
                top = new_top
            finish(slice(a * half, (a + 1) * half), top, total, acc)

    def settle(g, lane=0):
        def finish(cut, top, total, acc):
            att[lane, g, cut, :] = jnp.transpose(acc / total).astype(jnp.bfloat16)
        return finish

    def keep(g):
        def finish(cut, top, total, acc):
            own[g, :, cut] = acc
            own_stat[g, 0:1, cut] = top
            own_stat[g, 1:2, cut] = total
        return finish

    def hand_over(g, where):
        def finish(cut, top, total, acc):
            part_out[g, where, 0:HEAD_DIM, cut] = (acc / total).astype(jnp.bfloat16)
            level = top + jnp.log2(total)
            high = level.astype(jnp.bfloat16).astype(jnp.float32)
            middle = (level - high).astype(jnp.bfloat16).astype(jnp.float32)
            low = level - high - middle
            row = lax.broadcasted_iota(jnp.int32, (STAT, half), 0)
            stats = jnp.where(row == 0, high, jnp.where(row == 1, middle, jnp.where(row == 2, low, 0.0)))
            part_out[g, where, HEAD_DIM:HEAD_DIM + STAT, cut] = stats.astype(jnp.bfloat16)
        return finish

    def merge(g, slot=None, lane=0):
        slot = g if slot is None else slot
        pltpu.make_async_copy(part_in.at[slot], part_in.at[slot], part_recv.at[slot]).wait()
        for a in range(2):
            cut = slice(a * half, (a + 1) * half)
            stats = part_in[slot, HEAD_DIM:HEAD_DIM + STAT, cut].astype(jnp.float32)
            level = stats[0:1] + stats[1:2] + stats[2:3]
            top, total = own_stat[slot, 0:1, cut], own_stat[slot, 1:2, cut]
            new_top = jnp.maximum(top, level)
            mine, theirs = jnp.exp2(top - new_top), jnp.exp2(level - new_top)
            inverse = 1.0 / (total * mine + theirs)
            other = part_in[slot, 0:HEAD_DIM, cut].astype(jnp.float32)
            both = own[slot, :, cut] * (mine * inverse) + other * (theirs * inverse)
            att[lane, g, cut, :] = jnp.transpose(both).astype(jnp.bfloat16)

    def each(first, count, body):
        def step(g, carry):
            body(g)
            return carry
        lax.fori_loop(first, count, step, 0)

    upward = (*range(shared - 1), alone, shared - 1)

    @pl.when(s == 0)
    def _():
        for g in upward:
            scatter(K, g)
            scatter(V, g)
        for g in upward:
            scatter(Q, g)
        for g in upward:
            for kind in (K, V):
                arrived(kind, g, 0)
                line(kind, g, 1).start()

        def work(g):
            arrived(Q, g, 0)
            attend(g, 0, (), True, settle(g))
            give_back(g)
        each(0, group, work)

    @pl.when(s == 1)
    def _():
        scatter(K, alone)
        scatter(V, alone)
        for g in range(shared):
            scatter(K, g)
            scatter(V, g)
        for g in range(group):
            scatter(Q, g)
        for kind in (K, V):
            arrived(kind, alone, 1)
            line(kind, alone, 2).start()

        def far(g, last=3, slot=None):
            for kind in (K, V):
                arrived(kind, g, 1)
                arrived(kind, g, 0)
            for block in (2, 3):
                arrived(Q, g, block)
                attend(g, block, (0, 1), False, hand_over(g, block - n_seq // 2))
                if block == 3:
                    partial(g, block, last, slot).start()
                else:
                    partial(g, block).start()
        def near(g):
            arrived(Q, g, 1)
            attend(g, 1, (0,), True, settle(g))
            give_back(g)
        if guest == shared - 1:
            for kind in (K, V):
                arrived(kind, alone, 0)
                line(kind, alone, 2, 1, 0).start()
        far(guest, 2, visit)
        each(1, shared - 1, far)
        each(0, shared - 1, near)
        if guest < shared - 1:
            for kind in (K, V):
                arrived(kind, alone, 0)
                line(kind, alone, 2, 1, 0).start()
        each(alone, group, near)
        if guest < shared - 1:
            far(shared - 1)
        each(shared - 1, shared, near)

    @pl.when(s == 2)
    def _():
        for g in range(shared):
            scatter(Q, g)
        for g in (*range(1, shared), guest):
            scatter(K, g)
            scatter(V, g)
        for kind in (Q, K, V):
            scatter(kind, alone)
        for g in range(shared):
            arrived(Q, g, 2)
            line(Q, g, 1).start()
            arrived(Q, g, 3)
            line(Q, g, 1, 1, 3).start()
            if g > 0:
                for kind in (K, V):
                    arrived(kind, g, 2)
                    line(kind, g, 3).start()
        for kind in (K, V):
            arrived(kind, guest, 2)

        def near(g):
            attend(g, 2, (), True, keep(g))
        each(0, shared, near)
        for kind in (K, V):
            arrived(kind, guest, 3)
        attend(guest, 3, (2,), True, keep(visit))

        def join(g):
            merge(g)
            give_back(g)
        join(guest)
        for kind in (K, V):
            arrived(kind, alone, 1)
        for kind in (Q, K, V):
            arrived(kind, alone, 2)
        attend(alone, 2, (1,), True, keep(alone))
        merge(guest, visit, 1)
        give_back(guest, 1, 3)
        for kind in (Q, K, V):
            arrived(kind, alone, 3)
        attend(alone, 3, (1, 2), True, keep(late))
        each(1, shared - 1, join)
        for kind in (K, V):
            arrived(kind, alone, 0)
        attend(alone, 3, (0,), False, settle(alone, 1), late)
        give_back(alone, 1, 3)
        attend(alone, 2, (0,), False, settle(alone), alone)
        give_back(alone)
        each(max(1, shared - 1), shared, join)

    @pl.when(s == 3)
    def _():
        for g in range(shared):
            scatter(Q, g)
        for kind in (K, V):
            scatter(kind, guest)
        for g in range(1, shared):
            scatter(K, g)
            scatter(V, g)
        for kind in (Q, K, V):
            scatter(kind, alone)
        for g in range(shared):
            arrived(Q, g, 3)
            line(Q, g, 2).start()
        for kind in (K, V):
            arrived(kind, guest, 3)
            line(kind, guest, 2).start()
        for kind in (Q, K, V):
            arrived(kind, alone, 3)
            line(kind, alone, 2).start()

        def near(g):
            for kind in (K, V):
                arrived(kind, g, 3)
                arrived(kind, g, 2)
            attend(g, 3, (2,), True, keep(g))
        each(1, shared, near)

        def join(g):
            merge(g)
            give_back(g)
        each(1, shared, join)

    past_load.wait()
    weights = [table_ref[0, slot_ref[p]] + table_ref[1, slot_ref[p]] for p in range(past.shape[0])]

    def combine(g):
        for uly in range(n_uly):
            cols = columns(uly, g)
            pltpu.make_async_copy(back.at[:, cols], back.at[:, cols], back_sem.at[g, uly]).wait()
            mixed = back[:, cols].astype(jnp.float32)
            for p, weight in enumerate(weights):
                mixed = mixed + weight * past[p, :, cols].astype(jnp.float32)
            out_ref[:, cols] = mixed.astype(out_ref.dtype)
    each(0, group, combine)

    for g in range(group):
        for d in range(1, n_uly):
            for kind in (Q, K, V):
                plane(kind, g, d).wait_send()

    def returned(g, lane=0, block=None):
        for d in range(0 if block is not None else 1, n_uly):
            returning(g, lane, block, d).wait_send()

    @pl.when(s == 0)
    def _():
        for g in range(group):
            for kind in (K, V):
                line(kind, g, 1).wait_send()
            returned(g)

    @pl.when(s == 1)
    def _():
        for kind in (K, V):
            line(kind, alone, 2).wait_send()
            line(kind, alone, 2, 1, 0).wait_send()
        for g in range(shared):
            for block in (2, 3):
                partial(g, block).wait_send()
        for g in range(group):
            returned(g)

    @pl.when(s == 2)
    def _():
        for g in range(shared):
            line(Q, g, 1).wait_send()
            line(Q, g, 1, 1, 3).wait_send()
        for g in range(1, shared):
            for kind in (K, V):
                line(kind, g, 3).wait_send()
        for g in range(group):
            returned(g)
        for g in (guest, alone):
            returned(g, 1, 3)

    @pl.when(s == 3)
    def _():
        for g in range(shared):
            line(Q, g, 2).wait_send()
        for kind in (K, V):
            line(kind, guest, 2).wait_send()
        for g in range(1, shared):
            returned(g)
        for kind in (Q, K, V):
            line(kind, alone, 2).wait_send()


def fused(queries, keys, values, past_outputs, dwa_slot, dwa_table):
    n_seq, n_uly = lax.axis_size("seq"), lax.axis_size("uly")
    tokens, features = queries.shape
    group = features // n_uly // HEAD_DIM
    rows = tokens * n_uly
    stored = past_outputs.shape[0]
    bf16, f32 = jnp.bfloat16, jnp.float32
    anywhere = pl.BlockSpec(memory_space=pl.ANY)
    scalars = pl.BlockSpec(memory_space=pltpu.SMEM)
    return pl.pallas_call(
        functools.partial(fused_kernel, (n_seq, n_uly, group)),
        out_shape=jax.ShapeDtypeStruct((tokens, features), bf16),
        in_specs=[scalars, scalars, anywhere, anywhere, anywhere, anywhere],
        out_specs=pl.BlockSpec(memory_space=pltpu.VMEM),
        scratch_shapes=[
            pltpu.VMEM((3, tokens, features), bf16),
            pltpu.VMEM((stored, tokens, features), bf16),
            pltpu.VMEM((3, group, n_seq, rows, HEAD_DIM), bf16),
            pltpu.VMEM((group + 2, HEAD_DIM, rows), f32),
            pltpu.VMEM((group + 2, 8, rows), f32),
            pltpu.VMEM((group, 2, HEAD_DIM + STAT, rows), bf16),
            pltpu.VMEM((group + 2, HEAD_DIM + STAT, rows), bf16),
            pltpu.VMEM((2, group, rows, HEAD_DIM), bf16),
            pltpu.VMEM((tokens, features), bf16),
            pltpu.SemaphoreType.DMA((3,)),
            pltpu.SemaphoreType.DMA,
            pltpu.SemaphoreType.DMA((3, group, n_uly)),
            pltpu.SemaphoreType.DMA((3, group, 2)),
            pltpu.SemaphoreType.DMA((3, group, n_seq)),
            pltpu.SemaphoreType.DMA((group, 2)),
            pltpu.SemaphoreType.DMA((group + 2,)),
            pltpu.SemaphoreType.DMA((2, group, n_uly)),
            pltpu.SemaphoreType.DMA((group, n_uly)),
        ],
        compiler_params=pltpu.CompilerParams(
            collective_id=0, has_side_effects=True, vmem_limit_bytes=62 * 1024 * 1024
        ),
    )(dwa_slot, dwa_table, queries, keys, values, past_outputs)


def solution(mesh):
    def body(queries, *rest):
        heads_here = queries.shape[1] // HEAD_DIM // mesh.shape["uly"]
        fits = mesh.shape["seq"] == SPAN and heads_here >= 2
        return (fused if fits else shards)(queries, *rest)

    return jax.shard_map(
        body,
        mesh=mesh,
        in_specs=(
            P(("rep", "seq", "uly"), None),
            P(("rep", "seq", "uly"), None),
            P(("rep", "seq", "uly"), None),
            P(None, ("rep", "seq", "uly"), None),
            P(),
            P(),
        ),
        out_specs=P(("rep", "seq", "uly"), None),
        check_vma=False,
    )
```

profile of v0, /device:TPU:16, one launch (start us, length us, event | category | flops | bytes accessed | tf_op | source)
XLA Modules:
  0.0 49.4 jit_solution(17910245695502481137)
XLA Ops:
  0.0 47.5 %shard_map.64 = bf16[128,2048]{1,0:T(8,128)(2,1)} custom-call(s32[2]{0:T(128)} %slot_ref.1, f32[2,64]{1,0:T(2,128)} %table_ref.1, bf16[128,2048]{1,0:T(8,128)(2,1)} %q_hbm.1, bf16[128,2048]{1,0:T(8,128)(2,1)} %k_hbm.1, bf16[128,2048]{1,0:T(8,128)(2,1)} %v_hbm.1, bf16[2,128,2048]{2,1,0:T(8,128)(2,1)} %past_hbm.1), custom_call_target="tpu_custom_call" | custom-call | tf_op jit(solution)/shard_map/pallas_call | solution.py:489
  47.5 1.9 %copy.8 = bf16[128,2048]{1,0:T(8,128)(2,1)} copy(bf16[128,2048]{1,0:T(8,128)(2,1)} %shard_map.64) | data formatting | bytes 1048576
where the time goes:
time: 50.2 us; the launch traced here: 49.4 us
  Pallas kernels  47.5 us (95%)
  local copies, waits for them, and re-layouts  1.88 us (4%)
    pallas_call x1, Pallas kernels, fused(): pl.pallas_call(functools.partial(fused_kernel, (n_seq, n_uly, group)), ou...  47.5 us
    unnamed x1, local copies, waits for them, and re-layouts  1.88 us

commit v1 on v0

--- a/solution.py
+++ b/solution.py
@@ -91,8 +91,8 @@
 
 def fused_kernel(
     shape,
-    slot_ref, table_ref, q_hbm, k_hbm, v_hbm, past_hbm, out_ref,
-    given, past, heads, own, own_stat, part_out, part_in, att, back,
+    slot_ref, table_ref, q_hbm, k_hbm, v_hbm, past_hbm, back, base_ref,
+    given, past, heads, own, own_stat, part_out, part_in, att,
     load_sem, past_sem, plane_sem, line_sem, heads_sem, part_send, part_recv, att_sem, back_sem,
 ):
     n_seq, n_uly, group = shape
@@ -418,12 +418,17 @@
     def combine(g):
         for uly in range(n_uly):
             cols = columns(uly, g)
+            mixed = weights[0] * past[0, :, cols].astype(jnp.float32)
+            for p, weight in enumerate(weights[1:], 1):
+                mixed = mixed + weight * past[p, :, cols].astype(jnp.float32)
+            base_ref[:, cols] = mixed
+
+    def landed(g):
+        for uly in range(n_uly):
+            cols = columns(uly, g)
             pltpu.make_async_copy(back.at[:, cols], back.at[:, cols], back_sem.at[g, uly]).wait()
-            mixed = back[:, cols].astype(jnp.float32)
-            for p, weight in enumerate(weights):
-                mixed = mixed + weight * past[p, :, cols].astype(jnp.float32)
-            out_ref[:, cols] = mixed.astype(out_ref.dtype)
     each(0, group, combine)
+    each(0, group, landed)
 
     for g in range(group):
         for d in range(1, n_uly):
@@ -484,13 +489,13 @@
     rows = tokens * n_uly
     stored = past_outputs.shape[0]
     bf16, f32 = jnp.bfloat16, jnp.float32
-    anywhere = pl.BlockSpec(memory_space=pl.ANY)
+    anywhere = pl.BlockSpec(memory_space=pltpu.HBM)
     scalars = pl.BlockSpec(memory_space=pltpu.SMEM)
-    return pl.pallas_call(
+    attended, base = pl.pallas_call(
         functools.partial(fused_kernel, (n_seq, n_uly, group)),
-        out_shape=jax.ShapeDtypeStruct((tokens, features), bf16),
+        out_shape=(pltpu.VMEM((tokens, features), bf16), pltpu.VMEM((tokens, features), f32)),
         in_specs=[scalars, scalars, anywhere, anywhere, anywhere, anywhere],
-        out_specs=pl.BlockSpec(memory_space=pltpu.VMEM),
+        out_specs=[pl.BlockSpec(memory_space=pltpu.VMEM)] * 2,
         scratch_shapes=[
             pltpu.VMEM((3, tokens, features), bf16),
             pltpu.VMEM((stored, tokens, features), bf16),
@@ -500,7 +505,6 @@
             pltpu.VMEM((group, 2, HEAD_DIM + STAT, rows), bf16),
             pltpu.VMEM((group + 2, HEAD_DIM + STAT, rows), bf16),
             pltpu.VMEM((2, group, rows, HEAD_DIM), bf16),
-            pltpu.VMEM((tokens, features), bf16),
             pltpu.SemaphoreType.DMA((3,)),
             pltpu.SemaphoreType.DMA,
             pltpu.SemaphoreType.DMA((3, group, n_uly)),
@@ -512,9 +516,10 @@
             pltpu.SemaphoreType.DMA((group, n_uly)),
         ],
         compiler_params=pltpu.CompilerParams(
-            collective_id=0, has_side_effects=True, vmem_limit_bytes=62 * 1024 * 1024
+            collective_id=0, has_side_effects=True, vmem_limit_bytes=32 * 1024 * 1024
         ),
-    )(dwa_slot, dwa_table, queries, keys, values, past_outputs)
+    )(*(pltpu.with_memory_space_constraint(x, pltpu.HBM) for x in (dwa_slot, dwa_table, queries, keys, values, past_outputs)))
+    return (base + attended.astype(f32)).astype(bf16)
 
 
 def solution(mesh):

time: 50.2 us -> 48.2 us (0.960)
  local copies, waits for them, and re-layouts: 1.88 us -> 0 us
  Pallas kernels: 47.5 us -> 46.5 us
  other arithmetic: 0 us -> 0.9 us
    unnamed x1 -> x0, local copies, waits for them, and re-layouts: 1.88 us -> none
    pallas_call x1, Pallas kernels: 47.5 us -> 46.5 us  [fused(): pl.pallas_call(functools.partial(fused_kernel, (n_seq, n_uly, group)), ou...]
    convert_element_type x0 -> x1, other arithmetic: none -> 0.9 us  [fused(): return (base + attended.astype(f32)).astype(bf16)]
where the time goes in v1:
time: 48.2 us; the launch traced here: 47.4 us
  Pallas kernels  46.5 us (96%)
  other arithmetic  0.9 us (2%)
    pallas_call x1, Pallas kernels, fused(): pl.pallas_call(functools.partial(fused_kernel, (n_seq, n_uly, group)), ou...  46.5 us

profile of v1, /device:TPU:16, one launch (start us, length us, event | category | flops | bytes accessed | tf_op | source)
XLA Modules:
  0.0 47.4 jit_solution(15287260994534720784)
XLA Ops:
  0.0 46.5 %shard_map.64 = (bf16[128,2048]{1,0:T(8,128)(2,1)S(1)}, f32[128,2048]{1,0:T(8,128)S(1)}) custom-call(s32[2]{0:T(128)} %slot_ref.1, f32[2,64]{1,0:T(2,128)} %table_ref.1, bf16[128,2048]{1,0:T(8,128)(2,1)} %q_hbm.1, bf16[128,2048]{1,0:T(8,128)(2,1)} %k_hbm.1, bf16[128,2048]{1,0:T(8,128)(2,1)} %v_hbm.1, bf16[2,128,2048]{2,1,0:T(8,128)(2,1)} %past_hbm.1), custom_call_target="tpu_custom_call" | custom-call | tf_op jit(solution)/shard_map/pallas_call | solution.py:494
  46.5 0.9 %add_convert_fusion = bf16[128,2048]{1,0:T(8,128)(2,1)} fusion(f32[128,2048]{1,0:T(8,128)S(1)} %get-tuple-element.7, bf16[128,2048]{1,0:T(8,128)(2,1)S(1)} %get-tuple-element.8), kind=kLoop, calls=%fused_computation | loop fusion | flops 786432 | bytes 2097152 | tf_op jit(solution)/shard_map/convert_element_type | solution.py:522

commit v2 on v1

v2 whole, which is shorter than its diff:
```python
import functools
import math

import jax
import jax.numpy as jnp
from jax import lax
from jax.experimental import pallas as pl
from jax.experimental.pallas import tpu as pltpu
from jax.sharding import PartitionSpec as P

HEAD_DIM = 128
SPAN = 4
PLANE = 4
STAT = 8
MESH = pl.DeviceIdType.MESH
Q, K, V = 0, 1, 2


def from_behind(block, axis, distance):
    devices = range(lax.axis_size(axis))
    route = [(i - distance, i) for i in devices if i - distance in devices]
    return lax.ppermute(block, axis, route)


def block_update(state, query_heads, key_heads, value_heads, allowed):
    running, total, accumulated = state
    scores = jnp.einsum("qhd,khd->hqk", query_heads, key_heads, preferred_element_type=jnp.float32)
    scores = scores * (1.0 / HEAD_DIM**0.5)
    scores = jnp.where(allowed, scores, -jnp.inf)
    new_max = jnp.maximum(running, jnp.max(scores, axis=2))
    factor = jnp.exp(running - new_max)
    prob = jnp.exp(scores - new_max[:, :, None])
    total = total * factor + jnp.sum(prob, axis=2)
    weights = prob.astype(jnp.bfloat16)
    update = jnp.einsum("hqk,khd->qhd", weights, value_heads, preferred_element_type=jnp.float32)
    accumulated = accumulated * jnp.transpose(factor)[:, :, None] + update
    return (new_max, total, accumulated)


def shards(queries, keys, values, past_outputs, dwa_slot, dwa_table):
    n_uly = lax.axis_size("uly")
    n_seq = lax.axis_size("seq")
    span_size = min(4, n_seq)
    features = queries.shape[1]
    local_heads = features // n_uly // HEAD_DIM
    query_rows, key_rows, value_rows = (
        lax.all_to_all(queries, "uly", split_axis=1, concat_axis=0, tiled=True),
        lax.all_to_all(keys, "uly", split_axis=1, concat_axis=0, tiled=True),
        lax.all_to_all(values, "uly", split_axis=1, concat_axis=0, tiled=True),
    )
    row_count = query_rows.shape[0]
    split_shape = (row_count, local_heads, HEAD_DIM)
    query_heads = query_rows.reshape(split_shape)
    table_index = jnp.arange(dwa_table.shape[1])
    onehot = (dwa_slot[:, None] == table_index[None, :]).astype(jnp.float32)
    coefs = jnp.dot(onehot, jnp.transpose(dwa_table), precision=lax.Precision.HIGHEST)
    layer_in = jnp.zeros(queries.shape, jnp.float32)
    extra = jnp.zeros(queries.shape, jnp.float32)
    for index in range(past_outputs.shape[0]):
        stored = past_outputs[index].astype(jnp.float32)
        layer_in = layer_in + coefs[index, 0] * stored
        extra = extra + coefs[index, 1] * stored
    running = jnp.full((local_heads, row_count), -jnp.inf, jnp.float32)
    total = jnp.zeros((local_heads, row_count), jnp.float32)
    accumulated = jnp.zeros(split_shape, jnp.float32)
    state = (running, total, accumulated)
    causal = (jnp.arange(row_count)[:, None] >= jnp.arange(row_count)[None, :])[None, :, :]
    state = block_update(
        state, query_heads, key_rows.reshape(split_shape), value_rows.reshape(split_shape), causal
    )
    position = lax.axis_index("seq")
    current = (key_rows, value_rows)
    for offset in range(1, span_size):
        current = from_behind((current[0], current[1]), "seq", 1)
        far_keys = current[0].reshape(split_shape)
        far_values = current[1].reshape(split_shape)

        def take_block(carry, far_keys=far_keys, far_values=far_values):
            return block_update(carry, query_heads, far_keys, far_values, True)

        def keep_block(carry):
            return carry

        state = lax.cond(position >= offset, take_block, keep_block, state)
    running, total, accumulated = state
    attended = accumulated / jnp.transpose(total)[:, :, None]
    attended = attended.astype(jnp.bfloat16).reshape(row_count, local_heads * HEAD_DIM)
    returned = lax.all_to_all(attended, "uly", split_axis=0, concat_axis=1, tiled=True)
    hidden = layer_in + returned.astype(jnp.float32)
    return (hidden + extra).astype(jnp.bfloat16)


def fused_kernel(
    shape,
    slot_ref, table_ref, q_hbm, k_hbm, v_hbm, past_hbm, back, base_ref,
    given, past, heads, own, own_stat, part_out, part_in, att,
    load_sem, past_sem, plane_send, piece_sem, whole_sem, line_send, guest_send, line_recv,
    relay_sem, part_send, part_recv, att_send, back_sem,
):
    n_seq, n_uly, group = shape
    tokens = given.shape[1]
    rows = n_uly * tokens
    half = rows // 2
    scale = math.log2(math.e) / HEAD_DIM**0.5
    s, t = lax.axis_index("seq"), lax.axis_index("uly")
    y, x = t // 2, t % 2
    peers = (t, 2 * y + 1 - x, 2 * (1 - y) + x, 3 - t)
    guests = range(max(1, group // 2))
    hosts = range(len(guests), group)
    visit = group

    loads = [
        pltpu.make_async_copy(src, given.at[i], load_sem.at[i]) for i, src in enumerate((q_hbm, k_hbm, v_hbm))
    ]
    past_load = pltpu.make_async_copy(past_hbm, past, past_sem)
    for load in loads:
        load.start()
    past_load.start()

    barrier = pltpu.get_barrier_semaphore()
    for d in (1, 2, 3):
        pl.semaphore_signal(barrier, inc=1, device_id={"uly": peers[d]}, device_id_type=MESH)
    neighbours = {0: (1,), 1: (0, 2, 3), 2: (1, 3), 3: (1, 2)}
    for place, others in neighbours.items():
        @pl.when(s == place)
        def _(place=place, others=others):
            for other in others:
                pl.semaphore_signal(barrier, inc=1, device_id={"seq": other}, device_id_type=MESH)
            if place == 3:
                for d in (1, 2, 3):
                    pl.semaphore_signal(barrier, inc=1, device_id={"seq": 2, "uly": peers[d]}, device_id_type=MESH)
            pl.semaphore_wait(barrier, 3 + len(others) + (3 if place == 2 else 0))
    for load in loads:
        load.wait()

    def columns(uly, g):
        return pl.ds(pl.multiple_of((uly * group + g) * HEAD_DIM, HEAD_DIM), HEAD_DIM)

    def row_range(uly):
        return pl.ds(pl.multiple_of(uly * tokens, tokens), tokens)

    def scatter(kind, g, pieces):
        for d in (1, 2, 3, 0):
            src = given.at[kind, :, columns(peers[d], g)]
            dst = heads.at[kind, g, s, row_range(t), :]
            sem = piece_sem.at[kind, g, d] if pieces else whole_sem.at[kind, g]
            if d == 0:
                pltpu.make_async_copy(src, dst, sem).start()
            else:
                pltpu.make_async_remote_copy(
                    src, dst, plane_send.at[kind], sem, device_id={"uly": peers[d]}, device_id_type=MESH
                ).start()

    def landed(ref, sem):
        pltpu.make_async_copy(ref, ref, sem).wait()

    def gathered(kind, g):
        landed(heads.at[kind, g, s], whole_sem.at[kind, g])

    def gathered_piece(kind, g, d):
        landed(heads.at[kind, g, s, row_range(peers[d]), :], piece_sem.at[kind, g, d])

    def arrived(kind, g, block):
        landed(heads.at[kind, g, block], line_recv.at[kind, g, block])

    def pass_on(kind, g, d, to, guest=False):
        dst = heads.at[kind, g, s, row_range(peers[d]), :]
        src = given.at[kind, :, columns(t, g)] if d == 0 else dst
        sem = relay_sem.at[g, d] if to == 2 and kind == Q and g > 0 else line_recv.at[kind, g, s]
        pltpu.make_async_remote_copy(
            src, dst, guest_send if guest else line_send.at[kind], sem, device_id={"seq": to}, device_id_type=MESH
        ).start()

    def relay(g, d):
        ref = heads.at[Q, g, 3, row_range(peers[d]), :]
        landed(ref, relay_sem.at[g, d])
        pltpu.make_async_remote_copy(
            ref, ref, guest_send, line_recv.at[Q, g, 3], device_id={"seq": 1}, device_id_type=MESH
        ).start()

    def partial(g, where, a, to, slot):
        pltpu.make_async_remote_copy(
            part_out.at[g, where, a], part_in.at[slot, a], part_send, part_recv.at[slot, a],
            device_id={"seq": to}, device_id_type=MESH,
        ).start()

    def give_back(g, ds, lane=0):
        for d in ds:
            src = att.at[lane, g, row_range(peers[d]), :]
            dst = back.at[:, columns(t, g)]
            if lane == 0 and d == 0:
                pltpu.make_async_copy(src, dst, back_sem).start()
                continue
            where = {"uly": peers[d]} if lane == 0 else {"seq": n_seq - 1, "uly": peers[d]}
            pltpu.make_async_remote_copy(
                src, dst, att_send.at[lane], back_sem, device_id=where, device_id_type=MESH
            ).start()

    def attend_half(g, block, a, full, diagonal, finish, resume=None):
        query = heads[Q, g, block, pl.ds(pl.multiple_of(a * half, half), half), :]
        top = total = acc = None
        if resume is not None:
            top, total, acc = own_stat[resume, a, 0:1, :], own_stat[resume, a, 1:2, :], own[resume, a]
        spans = [(j, rows, False) for j in full] + ([(block, (a + 1) * half, True)] if diagonal else [])
        for j, count, masked in spans:
            key = heads[K, g, j, 0:count, :]
            value = heads[V, g, j, 0:count, :]
            scores = lax.dot_general(key, query, (((1,), (1,)), ((), ())), preferred_element_type=jnp.float32)
            scores = scores * scale
            if masked:
                key_at = lax.broadcasted_iota(jnp.int32, scores.shape, 0)
                query_at = lax.broadcasted_iota(jnp.int32, scores.shape, 1) + a * half
                scores = jnp.where(key_at <= query_at, scores, -jnp.inf)
            peak = jnp.max(scores, axis=0, keepdims=True)
            new_top = peak if top is None else jnp.maximum(top, peak)
            prob = jnp.exp2(scores - new_top)
            sums = jnp.sum(prob, axis=0, keepdims=True)
            update = lax.dot_general(
                value, prob.astype(jnp.bfloat16), (((0,), (0,)), ((), ())), preferred_element_type=jnp.float32
            )
            if top is None:
                total, acc = sums, update
            else:
                factor = jnp.exp2(top - new_top)
                total = total * factor + sums
                acc = acc * factor + update
            top = new_top
        finish(a, top, total, acc)

    def attend(g, block, full, diagonal, finish, resume=None):
        for a in range(2):
            attend_half(g, block, a, full, diagonal, finish, resume)

    def att_rows(a):
        return pl.ds(pl.multiple_of(a * half, half), half)

    def settle(g):
        def finish(a, top, total, acc):
            att[0, g, att_rows(a), :] = jnp.transpose(acc / total).astype(jnp.bfloat16)
        return finish

    def keep(slot):
        def finish(a, top, total, acc):
            own[slot, a] = acc
            own_stat[slot, a, 0:1, :] = top
            own_stat[slot, a, 1:2, :] = total
        return finish

    def hand_over(g, where):
        def finish(a, top, total, acc):
            part_out[g, where, a, 0:HEAD_DIM, :] = (acc / total).astype(jnp.bfloat16)
            level = top + jnp.log2(total)
            high = level.astype(jnp.bfloat16).astype(jnp.float32)
            middle = (level - high).astype(jnp.bfloat16).astype(jnp.float32)
            low = level - high - middle
            row = lax.broadcasted_iota(jnp.int32, (STAT, half), 0)
            stats = jnp.where(row == 0, high, jnp.where(row == 1, middle, jnp.where(row == 2, low, 0.0)))
            part_out[g, where, a, HEAD_DIM:HEAD_DIM + STAT, :] = stats.astype(jnp.bfloat16)
        return finish

    def merge(g, slot, a, lane=0):
        landed(part_in.at[slot, a], part_recv.at[slot, a])
        stats = part_in[slot, a, HEAD_DIM:HEAD_DIM + STAT, :].astype(jnp.float32)
        level = stats[0:1] + stats[1:2] + stats[2:3]
        top, total = own_stat[slot, a, 0:1, :], own_stat[slot, a, 1:2, :]
        new_top = jnp.maximum(top, level)
        mine, theirs = jnp.exp2(top - new_top), jnp.exp2(level - new_top)
        inverse = 1.0 / (total * mine + theirs)
        other = part_in[slot, a, 0:HEAD_DIM, :].astype(jnp.float32)
        both = own[slot, a] * (mine * inverse) + other * (theirs * inverse)
        att[lane, g, att_rows(a), :] = jnp.transpose(both).astype(jnp.bfloat16)

    def join(g, slot=None, lane=0):
        slot = g if slot is None else slot
        merge(g, slot, 1 - y, lane)
        give_back(g, (3, 2), lane)
        merge(g, slot, y, lane)
        give_back(g, (1, 0), lane)

    def each(first, count, body):
        def step(g, carry):
            body(g)
            return carry
        lax.fori_loop(first, count, step, 0)

    def add_up():
        past_load.wait()
        weights = [table_ref[0, slot_ref[p]] + table_ref[1, slot_ref[p]] for p in range(past.shape[0])]

        def sum_columns(uly):
            cols = pl.ds(pl.multiple_of(uly * (group * HEAD_DIM), HEAD_DIM), group * HEAD_DIM)
            mixed = weights[0] * past[0, :, cols].astype(jnp.float32)
            for p in range(1, past.shape[0]):
                mixed = mixed + weights[p] * past[p, :, cols].astype(jnp.float32)
            base_ref[:, cols] = mixed
        each(0, n_uly, sum_columns)

    def plane_sent():
        for kind in (Q, K, V):
            ref = given.at[kind, :, 0:(n_uly - 1) * group * HEAD_DIM]
            landed(ref, plane_send.at[kind])

    def line_sent(kind, first=0):
        landed(heads.at[kind, first:, s], line_send.at[kind])

    def att_sent(first=0):
        landed(att.at[0, first:, 0:(n_uly - 1) * tokens, :], att_send.at[0])

    @pl.when(s == 0)
    def _():
        for kind in (K, V):
            pass_on(kind, 0, 0, 1)
        for g in range(group):
            scatter(K, g, True)
            scatter(V, g, True)
        for g in range(group):
            scatter(Q, g, False)
        order = [(kind, g) for g in range(group) for kind in (K, V)]
        for i, (kind, g) in enumerate(order):
            if i + 2 < len(order):
                pass_on(*order[i + 2], 0, 1)
            for d in (1, 2, 3):
                gathered_piece(kind, g, d)
                pass_on(kind, g, d, 1)
        add_up()

        def work(g):
            gathered(Q, g)
            for kind in (K, V):
                gathered_piece(kind, g, 0)
            attend(g, 0, (), True, settle(g))
            give_back(g, (3, 2, 1, 0))
        each(0, group, work)
        plane_sent()
        for kind in (K, V):
            line_sent(kind)
        att_sent()

    @pl.when(s == 1)
    def _():
        for g in range(group):
            for kind in (K, V, Q):
                scatter(kind, g, False)
        add_up()

        def send(g, block, a):
            if block == 2:
                partial(g, 0, a, 2, g)
            else:
                stays = g < len(guests)
                partial(g, 1, a, jnp.where(stays, 2, 3), jnp.where(stays, visit + g, g))

        def far(g, block, full, resume=None):
            for a in (1 - y, y):
                attend_half(g, block, a, full, False, hand_over(g, block - 2), resume)
                send(g, block, a)

        def near(g):
            gathered(Q, g)
            attend(g, 1, (0,), True, settle(g))
            give_back(g, (3, 2, 1, 0))

        def both(g):
            for kind in (K, V):
                gathered(kind, g)
            for block in (3, 2):
                arrived(Q, g, block)
            for kind in (K, V):
                arrived(kind, g, 0)
            for block in (3, 2):
                far(g, block, (1, 0))

        for kind in (K, V):
            gathered(kind, 0)
        arrived(Q, 0, 2)
        attend(0, 2, (1,), False, keep(0))
        for kind in (K, V):
            arrived(kind, 0, 0)
        far(0, 2, (0,), 0)
        arrived(Q, 0, 3)
        far(0, 3, (1, 0))

        def work(g):
            near(g - 1)
            both(g)
        each(1, group, work)
        near(group - 1)
        plane_sent()
        landed(part_out, part_send)
        att_sent()

    @pl.when(s == 2)
    def _():
        pass_on(Q, 0, 0, 1)
        for kind in (K, V):
            pass_on(kind, hosts[0], 0, 3)
        order = [(Q, 0), (Q, 1)]
        for g in hosts:
            order += [(K, g), (V, g)] + ([(Q, g)] if g > 1 else [])
        order += [(Q, g) for g in range(2, hosts[0])]
        for kind, g in order:
            scatter(kind, g, True)
        for g in guests:
            for kind in (K, V):
                scatter(kind, g, False)
        for kind, g in order:
            to = 1 if kind == Q else 3
            if (g > 0 if kind == Q else g > hosts[0]):
                pass_on(kind, g, 0, to)
            for d in (1, 2, 3):
                gathered_piece(kind, g, d)
                pass_on(kind, g, d, to)
            if kind == Q and g > 0:
                for d in range(n_uly):
                    relay(g, d)
        add_up()

        def near(g):
            attend(g, 2, (), True, keep(g))

        def host(g):
            for kind in (Q, K, V):
                gathered_piece(kind, g, 0)
            near(g)

        def own_guest(g):
            for kind in (K, V):
                gathered(kind, g)
            gathered_piece(Q, g, 0)
            near(g)

        def receive(g):
            if g == 0:
                arrived(Q, g, 3)
            for kind in (K, V):
                arrived(kind, g, 3)
            attend(g, 3, (2,), True, keep(visit + g))

        each(hosts[0], group, host)
        each(0, len(guests), own_guest)
        receive(0)
        join(0)
        join(0, visit, 1)
        for g in guests[1:]:
            join(g)
            receive(g)
            join(g, visit + g, 1)
        each(hosts[0], group, join)
        plane_sent()
        line_sent(Q)
        for kind in (K, V):
            line_sent(kind, hosts[0])
        landed(heads.at[Q, 1:, 3], guest_send)
        landed(att.at[1, 0:len(guests)], att_send.at[1])
        att_sent()

    @pl.when(s == 3)
    def _():
        pass_on(Q, 0, 0, 1)
        pass_on(Q, 1, 0, 2)
        for g in range(group):
            scatter(Q, g, True)
        for g in guests:
            for kind in (K, V):
                scatter(kind, g, True)
        for g in hosts:
            for kind in (K, V):
                scatter(kind, g, False)
        for g in range(group):
            if g > 1:
                pass_on(Q, g, 0, 2)
            for d in (1, 2, 3):
                gathered_piece(Q, g, d)
                pass_on(Q, g, d, 2 if g > 0 else 1)
        for d in range(n_uly):
            pass_on(Q, 0, d, 2, True)
        for g in guests:
            for kind in (K, V):
                pass_on(kind, g, 0, 2)
                for d in (1, 2, 3):
                    gathered_piece(kind, g, d)
                    pass_on(kind, g, d, 2)
        for g in guests:
            for kind in (Q, K, V):
                gathered_piece(kind, g, 0)
        add_up()

        def near(g):
            gathered_piece(Q, g, 0)
            for kind in (K, V):
                gathered(kind, g)
                arrived(kind, g, 2)
            attend(g, 3, (2,), True, keep(g))
        each(hosts[0], group, near)
        each(hosts[0], group, join)
        plane_sent()
        line_sent(Q)
        for kind in (K, V):
            landed(heads.at[kind, 0:len(guests), s], line_send.at[kind])
        landed(heads.at[Q, 0, s], guest_send)
        att_sent(hosts[0])

    landed(back, back_sem)


def fused(queries, keys, values, past_outputs, dwa_slot, dwa_table):
    n_seq, n_uly = lax.axis_size("seq"), lax.axis_size("uly")
    tokens, features = queries.shape
    group = features // n_uly // HEAD_DIM
    rows = tokens * n_uly
    slots = group + max(1, group // 2)
    stored = past_outputs.shape[0]
    bf16, f32 = jnp.bfloat16, jnp.float32
    anywhere = pl.BlockSpec(memory_space=pltpu.HBM)
    scalars = pl.BlockSpec(memory_space=pltpu.SMEM)
    attended, base = pl.pallas_call(
        functools.partial(fused_kernel, (n_seq, n_uly, group)),
        out_shape=(pltpu.VMEM((tokens, features), bf16), pltpu.VMEM((tokens, features), f32)),
        in_specs=[scalars, scalars, anywhere, anywhere, anywhere, anywhere],
        out_specs=[pl.BlockSpec(memory_space=pltpu.VMEM)] * 2,
        scratch_shapes=[
            pltpu.VMEM((3, tokens, features), bf16),
            pltpu.VMEM((stored, tokens, features), bf16),
            pltpu.VMEM((3, group, n_seq, rows, HEAD_DIM), bf16),
            pltpu.VMEM((slots, 2, HEAD_DIM, rows // 2), f32),
            pltpu.VMEM((slots, 2, 8, rows // 2), f32),
            pltpu.VMEM((group, 2, 2, HEAD_DIM + STAT, rows // 2), bf16),
            pltpu.VMEM((slots, 2, HEAD_DIM + STAT, rows // 2), bf16),
            pltpu.VMEM((2, group, rows, HEAD_DIM), bf16),
            pltpu.SemaphoreType.DMA((3,)),
            pltpu.SemaphoreType.DMA,
            pltpu.SemaphoreType.DMA((3,)),
            pltpu.SemaphoreType.DMA((3, group, n_uly)),
            pltpu.SemaphoreType.DMA((3, group)),
            pltpu.SemaphoreType.DMA((3,)),
            pltpu.SemaphoreType.DMA,
            pltpu.SemaphoreType.DMA((3, group, n_seq)),
            pltpu.SemaphoreType.DMA((group, n_uly)),
            pltpu.SemaphoreType.DMA,
            pltpu.SemaphoreType.DMA((slots, 2)),
            pltpu.SemaphoreType.DMA((2,)),
            pltpu.SemaphoreType.DMA,
        ],
        compiler_params=pltpu.CompilerParams(
            collective_id=0, has_side_effects=True, vmem_limit_bytes=32 * 1024 * 1024
        ),
    )(*(pltpu.with_memory_space_constraint(x, pltpu.HBM) for x in (dwa_slot, dwa_table, queries, keys, values, past_outputs)))
    return (base + attended.astype(f32)).astype(bf16)


def solution(mesh):
    def body(queries, *rest):
        heads_here = queries.shape[1] // HEAD_DIM // mesh.shape["uly"]
        fits = mesh.shape["seq"] == SPAN and mesh.shape["uly"] == PLANE and heads_here >= 2
        return (fused if fits else shards)(queries, *rest)

    return jax.shard_map(
        body,
        mesh=mesh,
        in_specs=(
            P(("rep", "seq", "uly"), None),
            P(("rep", "seq", "uly"), None),
            P(("rep", "seq", "uly"), None),
            P(None, ("rep", "seq", "uly"), None),
            P(),
            P(),
        ),
        out_specs=P(("rep", "seq", "uly"), None),
        check_vma=False,
    )
```

time: 48.2 us -> 43.6 us (0.905); the launches traced: 47.4 us -> 43.4 us
  Pallas kernels: 46.5 us -> 42.5 us
    pallas_call x1, Pallas kernels: 46.5 us -> 42.5 us  [fused(): pl.pallas_call(functools.partial(fused_kernel, (n_seq, n_uly, group)), ou...]
where the time goes in v2:
time: 43.6 us; the launch traced here: 43.4 us
  Pallas kernels  42.5 us (97%)
  other arithmetic  0.9 us (2%)
    pallas_call x1, Pallas kernels, fused(): pl.pallas_call(functools.partial(fused_kernel, (n_seq, n_uly, group)), ou...  42.5 us
    convert_element_type x1, other arithmetic, fused(): return (base + attended.astype(f32)).astype(bf16)  0.9 us

profile of v2, /device:TPU:16, one launch (start us, length us, event | category | flops | bytes accessed | tf_op | source)
XLA Modules:
  0.0 43.4 jit_solution(8560432006689688601)
XLA Ops:
  0.0 42.5 %shard_map.64 = (bf16[128,2048]{1,0:T(8,128)(2,1)S(1)}, f32[128,2048]{1,0:T(8,128)S(1)}) custom-call(s32[2]{0:T(128)} %slot_ref.1, f32[2,64]{1,0:T(2,128)} %table_ref.1, bf16[128,2048]{1,0:T(8,128)(2,1)} %q_hbm.1, bf16[128,2048]{1,0:T(8,128)(2,1)} %k_hbm.1, bf16[128,2048]{1,0:T(8,128)(2,1)} %v_hbm.1, bf16[2,128,2048]{2,1,0:T(8,128)(2,1)} %past_hbm.1), custom_call_target="tpu_custom_call" | custom-call | tf_op jit(solution)/shard_map/pallas_call | solution.py:516
  42.5 0.9 %add_convert_fusion = bf16[128,2048]{1,0:T(8,128)(2,1)} fusion(f32[128,2048]{1,0:T(8,128)S(1)} %get-tuple-element.7, bf16[128,2048]{1,0:T(8,128)(2,1)S(1)} %get-tuple-element.8), kind=kLoop, calls=%fused_computation | loop fusion | flops 786432 | bytes 2097152 | tf_op jit(solution)/shard_map/convert_element_type | solution.py:548

commit v3 on v2

v3 whole, which is shorter than its diff:
```python
import functools
import math

import jax
import jax.numpy as jnp
from jax import lax
from jax.experimental import pallas as pl
from jax.experimental.pallas import tpu as pltpu
from jax.sharding import PartitionSpec as P

HEAD_DIM = 128
SPAN = 4
PLANE = 4
STAT = 8
MESH = pl.DeviceIdType.MESH
Q, K, V = 0, 1, 2


def from_behind(block, axis, distance):
    devices = range(lax.axis_size(axis))
    route = [(i - distance, i) for i in devices if i - distance in devices]
    return lax.ppermute(block, axis, route)


def block_update(state, query_heads, key_heads, value_heads, allowed):
    running, total, accumulated = state
    scores = jnp.einsum("qhd,khd->hqk", query_heads, key_heads, preferred_element_type=jnp.float32)
    scores = scores * (1.0 / HEAD_DIM**0.5)
    scores = jnp.where(allowed, scores, -jnp.inf)
    new_max = jnp.maximum(running, jnp.max(scores, axis=2))
    factor = jnp.exp(running - new_max)
    prob = jnp.exp(scores - new_max[:, :, None])
    total = total * factor + jnp.sum(prob, axis=2)
    weights = prob.astype(jnp.bfloat16)
    update = jnp.einsum("hqk,khd->qhd", weights, value_heads, preferred_element_type=jnp.float32)
    accumulated = accumulated * jnp.transpose(factor)[:, :, None] + update
    return (new_max, total, accumulated)


def shards(queries, keys, values, past_outputs, dwa_slot, dwa_table):
    n_uly = lax.axis_size("uly")
    n_seq = lax.axis_size("seq")
    span_size = min(4, n_seq)
    features = queries.shape[1]
    local_heads = features // n_uly // HEAD_DIM
    query_rows, key_rows, value_rows = (
        lax.all_to_all(queries, "uly", split_axis=1, concat_axis=0, tiled=True),
        lax.all_to_all(keys, "uly", split_axis=1, concat_axis=0, tiled=True),
        lax.all_to_all(values, "uly", split_axis=1, concat_axis=0, tiled=True),
    )
    row_count = query_rows.shape[0]
    split_shape = (row_count, local_heads, HEAD_DIM)
    query_heads = query_rows.reshape(split_shape)
    table_index = jnp.arange(dwa_table.shape[1])
    onehot = (dwa_slot[:, None] == table_index[None, :]).astype(jnp.float32)
    coefs = jnp.dot(onehot, jnp.transpose(dwa_table), precision=lax.Precision.HIGHEST)
    layer_in = jnp.zeros(queries.shape, jnp.float32)
    extra = jnp.zeros(queries.shape, jnp.float32)
    for index in range(past_outputs.shape[0]):
        stored = past_outputs[index].astype(jnp.float32)
        layer_in = layer_in + coefs[index, 0] * stored
        extra = extra + coefs[index, 1] * stored
    running = jnp.full((local_heads, row_count), -jnp.inf, jnp.float32)
    total = jnp.zeros((local_heads, row_count), jnp.float32)
    accumulated = jnp.zeros(split_shape, jnp.float32)
    state = (running, total, accumulated)
    causal = (jnp.arange(row_count)[:, None] >= jnp.arange(row_count)[None, :])[None, :, :]
    state = block_update(
        state, query_heads, key_rows.reshape(split_shape), value_rows.reshape(split_shape), causal
    )
    position = lax.axis_index("seq")
    current = (key_rows, value_rows)
    for offset in range(1, span_size):
        current = from_behind((current[0], current[1]), "seq", 1)
        far_keys = current[0].reshape(split_shape)
        far_values = current[1].reshape(split_shape)

        def take_block(carry, far_keys=far_keys, far_values=far_values):
            return block_update(carry, query_heads, far_keys, far_values, True)

        def keep_block(carry):
            return carry

        state = lax.cond(position >= offset, take_block, keep_block, state)
    running, total, accumulated = state
    attended = accumulated / jnp.transpose(total)[:, :, None]
    attended = attended.astype(jnp.bfloat16).reshape(row_count, local_heads * HEAD_DIM)
    returned = lax.all_to_all(attended, "uly", split_axis=0, concat_axis=1, tiled=True)
    hidden = layer_in + returned.astype(jnp.float32)
    return (hidden + extra).astype(jnp.bfloat16)


def fused_kernel(
    shape,
    slot_ref, table_ref, q_hbm, k_hbm, v_hbm, past_hbm, back, base_ref,
    given, past, heads, own, own_stat, part_out, part_in, att, last_out, last_in,
    load_sem, past_sem, plane_send, piece_sem, relay_sem, whole_sem, line_send, extra_send, line_recv,
    part_send, part_recv, att_send, back_sem, last_send, last_own, last_far,
):
    n_seq, n_uly, group = shape
    tokens = given.shape[1]
    rows = n_uly * tokens
    half = rows // 2
    scale = math.log2(math.e) / HEAD_DIM**0.5
    s, t = lax.axis_index("seq"), lax.axis_index("uly")
    y, x = t // 2, t % 2
    peers = (t, 2 * y + 1 - x, 2 * (1 - y) + x, 3 - t)
    guests = range(max(1, group // 2))
    hosts = range(len(guests), group)
    visit = group
    lanes = {(Q, 2): 0, (Q, 3): 1, (K, 0): 2, (V, 0): 3, (K, 2): 2, (V, 2): 3, (K, 3): 2, (V, 3): 3}

    loads = [
        pltpu.make_async_copy(src, given.at[i], load_sem) for i, src in enumerate((q_hbm, k_hbm, v_hbm))
    ]
    past_load = pltpu.make_async_copy(past_hbm, past, past_sem)
    for load in loads:
        load.start()
    past_load.start()

    def landed(ref, sem):
        pltpu.make_async_copy(ref, ref, sem).wait()

    barrier = pltpu.get_barrier_semaphore()
    for d in (1, 2, 3):
        pl.semaphore_signal(barrier, inc=1, device_id={"uly": peers[d]}, device_id_type=MESH)
    neighbours = {0: (1,), 1: (0, 2, 3), 2: (1, 3), 3: (1, 2)}
    for place, others in neighbours.items():
        @pl.when(s == place)
        def _(place=place, others=others):
            for other in others:
                pl.semaphore_signal(barrier, inc=1, device_id={"seq": other}, device_id_type=MESH)
            if place == 3:
                for d in (1, 2, 3):
                    pl.semaphore_signal(barrier, inc=1, device_id={"seq": 2, "uly": peers[d]}, device_id_type=MESH)
            pl.semaphore_wait(barrier, 3 + len(others) + (3 if place == 2 else 0))
    landed(given, load_sem)

    def columns(uly, g):
        return pl.ds(pl.multiple_of((uly * group + g) * HEAD_DIM, HEAD_DIM), HEAD_DIM)

    def row_range(uly):
        return pl.ds(pl.multiple_of(uly * tokens, tokens), tokens)

    def scatter(kind, g, pieces=None):
        for d in (1, 2, 3, 0):
            src = given.at[kind, :, columns(peers[d], g)]
            dst = heads.at[kind, g, s, row_range(t), :]
            sem = whole_sem.at[kind, g] if pieces is None else piece_sem.at[pieces, d]
            if d == 0:
                pltpu.make_async_copy(src, dst, sem).start()
            else:
                pltpu.make_async_remote_copy(
                    src, dst, plane_send, sem, device_id={"uly": peers[d]}, device_id_type=MESH
                ).start()

    def gathered(kind, g):
        landed(heads.at[kind, g, s], whole_sem.at[kind, g])

    def gathered_piece(kind, g, d, pieces):
        landed(heads.at[kind, g, s, row_range(peers[d]), :], piece_sem.at[pieces, d])

    def arrived(kind, g, block):
        landed(heads.at[kind, g, block], line_recv.at[lanes[kind, block], g])

    def pass_on(kind, g, d, block, to, send=None):
        dst = heads.at[kind, g, block, row_range(peers[d]), :]
        src = given.at[kind, :, columns(t, g)] if d == 0 else dst
        piecewise = kind == Q and block == 3 and to == 2 and g == 1
        sem = relay_sem.at[d] if piecewise else line_recv.at[lanes[kind, block], g]
        pltpu.make_async_remote_copy(
            src, dst, line_send.at[kind] if send is None else send, sem,
            device_id={"seq": to}, device_id_type=MESH,
        ).start()

    def forward(kind, g, block, to, pieces=None):
        if pieces is None:
            gathered(kind, g)
        for d in (1, 2, 3):
            if pieces is not None:
                gathered_piece(kind, g, d, pieces)
            pass_on(kind, g, d, block, to)

    def relay(g):
        parts = [heads.at[Q, g, 3]]
        if g == 1:
            parts = [heads.at[Q, g, 3, row_range(peers[d]), :] for d in range(n_uly)]
        for d, ref in enumerate(parts):
            landed(ref, relay_sem.at[d] if g == 1 else line_recv.at[lanes[Q, 3], g])
            pltpu.make_async_remote_copy(
                ref, ref, extra_send, line_recv.at[lanes[Q, 3], g], device_id={"seq": 1}, device_id_type=MESH
            ).start()

    def partial(g, where, a, to, slot):
        pltpu.make_async_remote_copy(
            part_out.at[g, where, a], part_in.at[slot, a], part_send, part_recv.at[slot, a],
            device_id={"seq": to}, device_id_type=MESH,
        ).start()

    def give_back(g, ds, lane=0):
        for d in ds:
            src = att.at[lane, g, row_range(peers[d]), :]
            dst = back.at[:, columns(t, g)]
            if lane == 0 and d == 0:
                pltpu.make_async_copy(src, dst, back_sem).start()
                continue
            where = {"uly": peers[d]} if lane == 0 else {"seq": n_seq - 1, "uly": peers[d]}
            pltpu.make_async_remote_copy(
                src, dst, att_send.at[lane], back_sem, device_id=where, device_id_type=MESH
            ).start()

    def attend(g, block, full, diagonal, finish, resume=None):
        query = heads[Q, g, block]
        acc_shape = (rows, HEAD_DIM)
        top = total = acc = None
        if resume is not None:
            top, total, acc = own_stat[resume, 0], own_stat[resume, 1], own[resume]
        for j in (*full, block) if diagonal else full:
            key = heads[K, g, j]
            value = heads[V, g, j]
            scores = lax.dot_general(query, key, (((1,), (1,)), ((), ())), preferred_element_type=jnp.float32)
            scores = scores * scale
            if j == block:
                query_at = lax.broadcasted_iota(jnp.int32, scores.shape, 0)
                key_at = lax.broadcasted_iota(jnp.int32, scores.shape, 1)
                scores = jnp.where(key_at <= query_at, scores, -jnp.inf)
            peak = jnp.broadcast_to(jnp.max(scores, axis=1, keepdims=True), acc_shape)
            new_top = peak if top is None else jnp.maximum(top, peak)
            prob = jnp.exp2(scores - jnp.concatenate([new_top] * (rows // HEAD_DIM), axis=1))
            sums = jnp.broadcast_to(jnp.sum(prob, axis=1, keepdims=True), acc_shape)
            update = jnp.dot(prob.astype(jnp.bfloat16), value, preferred_element_type=jnp.float32)
            if top is None:
                total, acc = sums, update
            else:
                factor = jnp.exp2(top - new_top)
                total = total * factor + sums
                acc = acc * factor + update
            top = new_top
        finish(top, total, acc)

    def settle(g):
        def finish(top, total, acc):
            att[0, g] = (acc / total).astype(jnp.bfloat16)
        return finish

    def keep(slot):
        def finish(top, total, acc):
            own[slot] = acc
            own_stat[slot, 0] = top
            own_stat[slot, 1] = total
        return finish

    def selector(shape, dim, chunk):
        place = lax.broadcasted_iota(jnp.int32, shape, dim) - 3 * chunk
        other = lax.broadcasted_iota(jnp.int32, shape, 1 - dim)
        return place, other

    def packed(top, total):
        level = top + jnp.log2(total)
        high = level.astype(jnp.bfloat16).astype(jnp.float32)
        middle = (level - high).astype(jnp.bfloat16).astype(jnp.float32)
        low = level - high - middle
        lane = lax.broadcasted_iota(jnp.int32, (rows, HEAD_DIM), 1)
        split = jnp.where(lane == 0, high, jnp.where(lane == 1, middle, jnp.where(lane == 2, low, 0.0)))
        return split.astype(jnp.bfloat16)

    def turned(split, first, chunk):
        place, other = selector((STAT, HEAD_DIM), 0, chunk)
        pick = jnp.where((place == other) & (other < 3), 1.0, 0.0).astype(jnp.bfloat16)
        return lax.dot_general(
            pick, split[first:first + HEAD_DIM], (((1,), (1,)), ((), ())), preferred_element_type=jnp.float32
        )

    def level_of(stats, chunk):
        place, _ = selector((STAT, HEAD_DIM), 0, chunk)
        ones = jnp.where((place >= 0) & (place < 3), 1.0, 0.0).astype(jnp.bfloat16)
        return lax.dot_general(stats, ones, (((0,), (0,)), ((), ())), preferred_element_type=jnp.float32)

    def hand_over(g, where):
        def finish(top, total, acc):
            result = (acc / total).astype(jnp.bfloat16)
            split = packed(top, total)
            for a in range(2):
                part_out[g, where, a, 0:half, :] = result[a * half:(a + 1) * half]
                stats = turned(split, a * half, 0) + turned(split, a * half + HEAD_DIM, 1)
                part_out[g, where, a, half:half + STAT, :] = stats.astype(jnp.bfloat16)
        return finish

    def hand_out(where):
        def finish(top, total, acc):
            result = (acc / total).astype(jnp.bfloat16)
            split = packed(top, total)
            for u in range(n_uly):
                last_out[where, u, 0:tokens, :] = result[u * tokens:(u + 1) * tokens]
                last_out[where, u, tokens:tokens + STAT, :] = turned(split, u * tokens, 0).astype(jnp.bfloat16)
        return finish

    def send_last(where, far, block=None):
        for d in (3, 2, 1, 0):
            src, dst = last_out.at[where, peers[d]], last_in.at[1 if far else 0, t]
            if d == 0 and not far:
                pltpu.make_async_copy(src, dst, last_own).start()
                continue
            place = {"uly": peers[d]} if block is None else {"seq": block, "uly": peers[d]}
            pltpu.make_async_remote_copy(
                src, dst, last_send, last_far.at[t] if far else last_own, device_id=place, device_id_type=MESH
            ).start()

    def join_last():
        landed(last_in.at[0], last_own)
        for d in range(n_uly):
            u = peers[d]
            landed(last_in.at[1, u], last_far.at[u])
            mine = level_of(last_in[0, u, tokens:tokens + STAT, :], 0)
            theirs = level_of(last_in[1, u, tokens:tokens + STAT, :], 0)
            top = jnp.maximum(mine, theirs)
            mine, theirs = jnp.exp2(mine - top), jnp.exp2(theirs - top)
            first = last_in[0, u, 0:tokens, :].astype(jnp.float32)
            second = last_in[1, u, 0:tokens, :].astype(jnp.float32)
            both = (first * mine + second * theirs) / (mine + theirs)
            back[:, columns(u, group - 1)] = both.astype(jnp.bfloat16)
        landed(back.at[:, 0:(group - 1) * n_uly * HEAD_DIM], back_sem)

    def merge(g, slot, a, lane=0):
        landed(part_in.at[slot, a], part_recv.at[slot, a])
        stats = part_in[slot, a, half:half + STAT, :]
        for chunk in range(2):
            level = level_of(stats, chunk)
            first = pl.multiple_of(a * half + chunk * HEAD_DIM, HEAD_DIM)
            cut = pl.ds(first, HEAD_DIM)
            top, total = own_stat[slot, 0, cut, :], own_stat[slot, 1, cut, :]
            new_top = jnp.maximum(top, level)
            mine, theirs = jnp.exp2(top - new_top), jnp.exp2(level - new_top)
            inverse = 1.0 / (total * mine + theirs)
            other = part_in[slot, a, chunk * HEAD_DIM:(chunk + 1) * HEAD_DIM, :].astype(jnp.float32)
            both = own[slot, cut, :] * (mine * inverse) + other * (theirs * inverse)
            att[lane, g, cut, :] = both.astype(jnp.bfloat16)

    def join(g, slot=None, lane=0):
        slot = g if slot is None else slot
        merge(g, slot, 1 - y, lane)
        give_back(g, (3, 2), lane)
        merge(g, slot, y, lane)
        give_back(g, (1, 0), lane)

    def each(first, count, body):
        def step(g, carry):
            body(g)
            return carry
        lax.fori_loop(first, count, step, 0)

    def add_up():
        past_load.wait()
        weights = [table_ref[0, slot_ref[p]] + table_ref[1, slot_ref[p]] for p in range(past.shape[0])]

        def sum_columns(uly):
            cols = pl.ds(pl.multiple_of(uly * (group * HEAD_DIM), HEAD_DIM), group * HEAD_DIM)
            mixed = weights[0] * past[0, :, cols].astype(jnp.float32)
            for p in range(1, past.shape[0]):
                mixed = mixed + weights[p] * past[p, :, cols].astype(jnp.float32)
            base_ref[:, cols] = mixed
        each(0, n_uly, sum_columns)

    def plane_sent():
        landed(given.at[:, :, 0:(n_uly - 1) * group * HEAD_DIM], plane_send)

    def line_sent(kind, block, first=0, count=group):
        landed(heads.at[kind, first:count, block], line_send.at[kind])

    def att_sent(first=0, count=group):
        if count > first:
            landed(att.at[0, first:count, 0:(n_uly - 1) * tokens, :], att_send.at[0])

    @pl.when(s == 0)
    def _():
        for kind in (K, V):
            pass_on(kind, 0, 0, 0, 1)
        order = [(kind, g) for g in range(group) for kind in (K, V)]
        for i, (kind, g) in enumerate(order):
            scatter(kind, g, i if g == 0 else None)
        for g in range(group):
            scatter(Q, g)
        for i, (kind, g) in enumerate(order):
            if i + 2 < len(order):
                pass_on(*order[i + 2], 0, 0, 1)
            forward(kind, g, 0, 1, i if g == 0 else None)
        for i in range(2):
            gathered_piece(*order[i], 0, i)
        add_up()

        def work(g):
            gathered(Q, g)
            attend(g, 0, (), True, settle(g))
            give_back(g, (3, 2, 1, 0))
        each(0, group, work)
        plane_sent()
        for kind in (K, V):
            line_sent(kind, 0)
        att_sent()
        landed(back, back_sem)

    @pl.when(s == 1)
    def _():
        for g in range(group):
            for kind in (K, V, Q):
                scatter(kind, g)
        add_up()

        def nearest(g):
            for kind in (K, V):
                gathered(kind, g)
            for block in (2, 3):
                arrived(Q, g, block)
                attend(g, block, (1,), False, keep(block - 2))
            for kind in (K, V):
                arrived(kind, g, 0)

        def near(g):
            gathered(Q, g)
            attend(g, 1, (0,), True, settle(g))
            give_back(g, (3, 2, 1, 0))

        def work(g):
            nearest(g)
            stays = g < len(guests)
            attend(g, 3, (0,), False, hand_over(g, 1), 1)
            for a in (1 - y, y):
                partial(g, 1, a, jnp.where(stays, 2, 3), jnp.where(stays, visit + g, g))
            attend(g, 2, (0,), False, hand_over(g, 0), 0)
            for a in (1 - y, y):
                partial(g, 0, a, 2, g)
            near(g)
        each(0, group - 1, work)
        nearest(group - 1)
        for block in (3, 2):
            attend(group - 1, block, (0,), False, hand_out(block - 2), block - 2)
            send_last(block - 2, True, block)
        near(group - 1)
        plane_sent()
        landed(part_out, part_send)
        landed(last_out, last_send)
        att_sent()
        landed(back, back_sem)

    @pl.when(s == 2)
    def _():
        pass_on(Q, 0, 0, 2, 1)
        for kind in (K, V):
            pass_on(kind, hosts[0], 0, 2, 3)
        order = [(Q, 0), (Q, 1)]
        for g in hosts:
            order += [(K, g), (V, g)] + ([(Q, g)] if g > 1 else [])
        order += [(Q, g) for g in range(2, hosts[0])]
        for kind, g in order:
            scatter(kind, g, g if kind == Q and g < 2 else None)
        for g in guests:
            for kind in (K, V):
                scatter(kind, g)
        for kind, g in order:
            to = 1 if kind == Q else 3
            if (g > 0 if kind == Q else g > hosts[0]):
                pass_on(kind, g, 0, 2, to)
            forward(kind, g, 2, to, g if kind == Q and g < 2 else None)
            if kind == Q and g > 0:
                relay(g)
        for g in range(2):
            gathered_piece(Q, g, 0, g)
        add_up()

        def near(g):
            attend(g, 2, (), True, keep(g))

        def own_guest(g):
            for kind in (K, V):
                gathered(kind, g)
            near(g)

        def receive(g):
            if g == 0:
                arrived(Q, g, 3)
            for kind in (K, V):
                arrived(kind, g, 3)
            attend(g, 3, (2,), True, keep(visit + g))

        attend(group - 1, 2, (), True, hand_out(0))
        send_last(0, False)
        each(hosts[0], group - 1, near)
        each(0, len(guests), own_guest)
        receive(0)
        join(0)
        join(0, visit, 1)
        for g in guests[1:]:
            join(g)
            receive(g)
            join(g, visit + g, 1)
        each(hosts[0], group - 1, join)
        plane_sent()
        line_sent(Q, 2)
        for kind in (K, V):
            line_sent(kind, 2, hosts[0])
        landed(heads.at[Q, 1:, 3], extra_send)
        landed(last_out.at[0, 0:n_uly - 1], last_send)
        landed(att.at[1, 0:len(guests)], att_send.at[1])
        att_sent(0, group - 1)
        join_last()

    @pl.when(s == 3)
    def _():
        pass_on(Q, 0, 0, 3, 1)
        pass_on(Q, 1, 0, 3, 2)
        for g in range(group):
            scatter(Q, g, g if g < 2 else None)
        for g in (*guests, *hosts):
            for kind in (K, V):
                scatter(kind, g)
        for g in range(group):
            if g > 1:
                pass_on(Q, g, 0, 3, 2)
            forward(Q, g, 3, 2 if g > 0 else 1, g if g < 2 else None)
        for d in range(n_uly):
            pass_on(Q, 0, d, 3, 2, extra_send)
        for g in guests:
            for kind in (K, V):
                pass_on(kind, g, 0, 3, 2)
                forward(kind, g, 3, 2)
        for g in range(2):
            gathered_piece(Q, g, 0, g)
        add_up()

        def near(g, finish=None):
            for kind in (K, V):
                gathered(kind, g)
                arrived(kind, g, 2)
            attend(g, 3, (2,), True, keep(g) if finish is None else finish)
        each(hosts[0], group - 1, near)
        near(group - 1, hand_out(0))
        send_last(0, False)
        each(hosts[0], group - 1, join)
        plane_sent()
        line_sent(Q, 3)
        for kind in (K, V):
            line_sent(kind, 3, 0, len(guests))
        landed(heads.at[Q, 0, 3], extra_send)
        landed(last_out.at[0, 0:n_uly - 1], last_send)
        att_sent(hosts[0], group - 1)
        join_last()


def fused(queries, keys, values, past_outputs, dwa_slot, dwa_table):
    n_seq, n_uly = lax.axis_size("seq"), lax.axis_size("uly")
    tokens, features = queries.shape
    group = features // n_uly // HEAD_DIM
    rows = tokens * n_uly
    slots = group + max(1, group // 2)
    stored = past_outputs.shape[0]
    bf16, f32 = jnp.bfloat16, jnp.float32
    anywhere = pl.BlockSpec(memory_space=pltpu.HBM)
    scalars = pl.BlockSpec(memory_space=pltpu.SMEM)
    attended, base = pl.pallas_call(
        functools.partial(fused_kernel, (n_seq, n_uly, group)),
        out_shape=(pltpu.VMEM((tokens, features), bf16), pltpu.VMEM((tokens, features), f32)),
        in_specs=[scalars, scalars, anywhere, anywhere, anywhere, anywhere],
        out_specs=[pl.BlockSpec(memory_space=pltpu.VMEM)] * 2,
        scratch_shapes=[
            pltpu.VMEM((3, tokens, features), bf16),
            pltpu.VMEM((stored, tokens, features), bf16),
            pltpu.VMEM((3, group, n_seq, rows, HEAD_DIM), bf16),
            pltpu.VMEM((slots, rows, HEAD_DIM), f32),
            pltpu.VMEM((slots, 2, rows, HEAD_DIM), f32),
            pltpu.VMEM((group - 1, 2, 2, rows // 2 + STAT, HEAD_DIM), bf16),
            pltpu.VMEM((slots, 2, rows // 2 + STAT, HEAD_DIM), bf16),
            pltpu.VMEM((2, group, rows, HEAD_DIM), bf16),
            pltpu.VMEM((2, n_uly, tokens + STAT, HEAD_DIM), bf16),
            pltpu.VMEM((2, n_uly, tokens + STAT, HEAD_DIM), bf16),
            pltpu.SemaphoreType.DMA,
            pltpu.SemaphoreType.DMA,
            pltpu.SemaphoreType.DMA,
            pltpu.SemaphoreType.DMA((2, n_uly)),
            pltpu.SemaphoreType.DMA((n_uly,)),
            pltpu.SemaphoreType.DMA((3, group)),
            pltpu.SemaphoreType.DMA((3,)),
            pltpu.SemaphoreType.DMA,
            pltpu.SemaphoreType.DMA((4, group)),
            pltpu.SemaphoreType.DMA,
            pltpu.SemaphoreType.DMA((slots, 2)),
            pltpu.SemaphoreType.DMA((2,)),
            pltpu.SemaphoreType.DMA,
            pltpu.SemaphoreType.DMA,
            pltpu.SemaphoreType.DMA,
            pltpu.SemaphoreType.DMA((n_uly,)),
        ],
        compiler_params=pltpu.CompilerParams(
            collective_id=0, has_side_effects=True, vmem_limit_bytes=32 * 1024 * 1024
        ),
    )(*(pltpu.with_memory_space_constraint(x, pltpu.HBM) for x in (dwa_slot, dwa_table, queries, keys, values, past_outputs)))
    return (base + attended.astype(f32)).astype(bf16)


def solution(mesh):
    def body(queries, *rest):
        heads_here = queries.shape[1] // HEAD_DIM // mesh.shape["uly"]
        fits = mesh.shape["seq"] == SPAN and mesh.shape["uly"] == PLANE and heads_here >= 2
        return (fused if fits else shards)(queries, *rest)

    return jax.shard_map(
        body,
        mesh=mesh,
        in_specs=(
            P(("rep", "seq", "uly"), None),
            P(("rep", "seq", "uly"), None),
            P(("rep", "seq", "uly"), None),
            P(None, ("rep", "seq", "uly"), None),
            P(),
            P(),
        ),
        out_specs=P(("rep", "seq", "uly"), None),
        check_vma=False,
    )
```

time: 43.6 us -> 41 us (0.940)
  Pallas kernels: 42.5 us -> 39.9 us
    pallas_call x1, Pallas kernels: 42.5 us -> 39.9 us  [fused(): pl.pallas_call(functools.partial(fused_kernel, (n_seq, n_uly, group)), ou...]
where the time goes in v3:
time: 41 us; the launch traced here: 40.8 us
  Pallas kernels  39.9 us (97%)
  other arithmetic  0.9 us (2%)
    pallas_call x1, Pallas kernels, fused(): pl.pallas_call(functools.partial(fused_kernel, (n_seq, n_uly, group)), ou...  39.9 us
    convert_element_type x1, other arithmetic, fused(): return (base + attended.astype(f32)).astype(bf16)  0.9 us

profile of v3, /device:TPU:16, one launch (start us, length us, event | category | flops | bytes accessed | tf_op | source)
XLA Modules:
  0.0 40.8 jit_solution(1010878558636177221)
XLA Ops:
  0.0 39.9 %shard_map.64 = (bf16[128,2048]{1,0:T(8,128)(2,1)S(1)}, f32[128,2048]{1,0:T(8,128)S(1)}) custom-call(s32[2]{0:T(128)} %slot_ref.1, f32[2,64]{1,0:T(2,128)} %table_ref.1, bf16[128,2048]{1,0:T(8,128)(2,1)} %q_hbm.1, bf16[128,2048]{1,0:T(8,128)(2,1)} %k_hbm.1, bf16[128,2048]{1,0:T(8,128)(2,1)} %v_hbm.1, bf16[2,128,2048]{2,1,0:T(8,128)(2,1)} %past_hbm.1), custom_call_target="tpu_custom_call" | custom-call | tf_op jit(solution)/shard_map/pallas_call | solution.py:559
  39.9 0.9 %add_convert_fusion = bf16[128,2048]{1,0:T(8,128)(2,1)} fusion(f32[128,2048]{1,0:T(8,128)S(1)} %get-tuple-element.7, bf16[128,2048]{1,0:T(8,128)(2,1)S(1)} %get-tuple-element.8), kind=kLoop, calls=%fused_computation | loop fusion | flops 786432 | bytes 2097152 | tf_op jit(solution)/shard_map/convert_element_type | solution.py:596

commit v4 on v3

--- a/solution.py
+++ b/solution.py
@@ -92,9 +92,9 @@
 
 def fused_kernel(
     shape,
-    slot_ref, table_ref, q_hbm, k_hbm, v_hbm, past_hbm, back, base_ref,
-    given, past, heads, own, own_stat, part_out, part_in, att, last_out, last_in,
-    load_sem, past_sem, plane_send, piece_sem, relay_sem, whole_sem, line_send, extra_send, line_recv,
+    slot_hbm, table_hbm, q_hbm, k_hbm, v_hbm, past_hbm, back, base_ref,
+    slot_ref, table_ref, given, past, heads, own, own_stat, part_out, part_in, att, last_out, last_in,
+    load_sem, past_sem, table_sem, plane_send, piece_sem, relay_sem, whole_sem, line_send, extra_send, line_recv,
     part_send, part_recv, att_send, back_sem, last_send, last_own, last_far,
 ):
     n_seq, n_uly, group = shape
@@ -113,10 +113,13 @@
     loads = [
         pltpu.make_async_copy(src, given.at[i], load_sem) for i, src in enumerate((q_hbm, k_hbm, v_hbm))
     ]
+    table_loads = [
+        pltpu.make_async_copy(src, dst, table_sem.at[i])
+        for i, (src, dst) in enumerate(((slot_hbm, slot_ref), (table_hbm, table_ref)))
+    ]
     past_load = pltpu.make_async_copy(past_hbm, past, past_sem)
-    for load in loads:
+    for load in (*loads, past_load, *table_loads):
         load.start()
-    past_load.start()
 
     def landed(ref, sem):
         pltpu.make_async_copy(ref, ref, sem).wait()
@@ -163,13 +166,13 @@
     def arrived(kind, g, block):
         landed(heads.at[kind, g, block], line_recv.at[lanes[kind, block], g])
 
-    def pass_on(kind, g, d, block, to, send=None):
+    def pass_on(kind, g, d, block, to):
         dst = heads.at[kind, g, block, row_range(peers[d]), :]
         src = given.at[kind, :, columns(t, g)] if d == 0 else dst
-        piecewise = kind == Q and block == 3 and to == 2 and g == 1
-        sem = relay_sem.at[d] if piecewise else line_recv.at[lanes[kind, block], g]
+        piecewise = kind == Q and block == 3 and g < 2
+        sem = relay_sem.at[g, d] if piecewise else line_recv.at[lanes[kind, block], g]
         pltpu.make_async_remote_copy(
-            src, dst, line_send.at[kind] if send is None else send, sem,
+            src, dst, line_send.at[kind], sem,
             device_id={"seq": to}, device_id_type=MESH,
         ).start()
 
@@ -183,10 +186,10 @@
 
     def relay(g):
         parts = [heads.at[Q, g, 3]]
-        if g == 1:
+        if g < 2:
             parts = [heads.at[Q, g, 3, row_range(peers[d]), :] for d in range(n_uly)]
         for d, ref in enumerate(parts):
-            landed(ref, relay_sem.at[d] if g == 1 else line_recv.at[lanes[Q, 3], g])
+            landed(ref, relay_sem.at[g, d] if g < 2 else line_recv.at[lanes[Q, 3], g])
             pltpu.make_async_remote_copy(
                 ref, ref, extra_send, line_recv.at[lanes[Q, 3], g], device_id={"seq": 1}, device_id_type=MESH
             ).start()
@@ -350,7 +353,8 @@
         lax.fori_loop(first, count, step, 0)
 
     def add_up():
-        past_load.wait()
+        for load in (past_load, *table_loads):
+            load.wait()
         weights = [table_ref[0, slot_ref[p]] + table_ref[1, slot_ref[p]] for p in range(past.shape[0])]
 
         def sum_columns(uly):
@@ -406,14 +410,16 @@
                 scatter(kind, g)
         add_up()
 
-        def nearest(g):
-            for kind in (K, V):
-                gathered(kind, g)
-            for block in (2, 3):
-                arrived(Q, g, block)
-                attend(g, block, (1,), False, keep(block - 2))
-            for kind in (K, V):
-                arrived(kind, g, 0)
+        def far(g, block, finish):
+            if block == 2:
+                for kind in (K, V):
+                    gathered(kind, g)
+            arrived(Q, g, block)
+            attend(g, block, (1,), False, keep(block - 2))
+            if block == 2:
+                for kind in (K, V):
+                    arrived(kind, g, 0)
+            attend(g, block, (0,), False, finish, block - 2)
 
         def near(g):
             gathered(Q, g)
@@ -421,19 +427,17 @@
             give_back(g, (3, 2, 1, 0))
 
         def work(g):
-            nearest(g)
+            far(g, 2, hand_over(g, 0))
+            for a in (1 - y, y):
+                partial(g, 0, a, 2, g)
+            far(g, 3, hand_over(g, 1))
             stays = g < len(guests)
-            attend(g, 3, (0,), False, hand_over(g, 1), 1)
             for a in (1 - y, y):
                 partial(g, 1, a, jnp.where(stays, 2, 3), jnp.where(stays, visit + g, g))
-            attend(g, 2, (0,), False, hand_over(g, 0), 0)
-            for a in (1 - y, y):
-                partial(g, 0, a, 2, g)
             near(g)
         each(0, group - 1, work)
-        nearest(group - 1)
-        for block in (3, 2):
-            attend(group - 1, block, (0,), False, hand_out(block - 2), block - 2)
+        for block in (2, 3):
+            far(group - 1, block, hand_out(block - 2))
             send_last(block - 2, True, block)
         near(group - 1)
         plane_sent()
@@ -461,7 +465,7 @@
             if (g > 0 if kind == Q else g > hosts[0]):
                 pass_on(kind, g, 0, 2, to)
             forward(kind, g, 2, to, g if kind == Q and g < 2 else None)
-            if kind == Q and g > 0:
+            if kind == Q:
                 relay(g)
         for g in range(2):
             gathered_piece(Q, g, 0, g)
@@ -476,8 +480,6 @@
             near(g)
 
         def receive(g):
-            if g == 0:
-                arrived(Q, g, 3)
             for kind in (K, V):
                 arrived(kind, g, 3)
             attend(g, 3, (2,), True, keep(visit + g))
@@ -498,7 +500,7 @@
         line_sent(Q, 2)
         for kind in (K, V):
             line_sent(kind, 2, hosts[0])
-        landed(heads.at[Q, 1:, 3], extra_send)
+        landed(heads.at[Q, :, 3], extra_send)
         landed(last_out.at[0, 0:n_uly - 1], last_send)
         landed(att.at[1, 0:len(guests)], att_send.at[1])
         att_sent(0, group - 1)
@@ -506,8 +508,8 @@
 
     @pl.when(s == 3)
     def _():
-        pass_on(Q, 0, 0, 3, 1)
-        pass_on(Q, 1, 0, 3, 2)
+        for g in range(2):
+            pass_on(Q, g, 0, 3, 2)
         for g in range(group):
             scatter(Q, g, g if g < 2 else None)
         for g in (*guests, *hosts):
@@ -516,9 +518,7 @@
         for g in range(group):
             if g > 1:
                 pass_on(Q, g, 0, 3, 2)
-            forward(Q, g, 3, 2 if g > 0 else 1, g if g < 2 else None)
-        for d in range(n_uly):
-            pass_on(Q, 0, d, 3, 2, extra_send)
+            forward(Q, g, 3, 2, g if g < 2 else None)
         for g in guests:
             for kind in (K, V):
                 pass_on(kind, g, 0, 3, 2)
@@ -540,7 +540,6 @@
         line_sent(Q, 3)
         for kind in (K, V):
             line_sent(kind, 3, 0, len(guests))
-        landed(heads.at[Q, 0, 3], extra_send)
         landed(last_out.at[0, 0:n_uly - 1], last_send)
         att_sent(hosts[0], group - 1)
         join_last()
@@ -555,13 +554,14 @@
     stored = past_outputs.shape[0]
     bf16, f32 = jnp.bfloat16, jnp.float32
     anywhere = pl.BlockSpec(memory_space=pltpu.HBM)
-    scalars = pl.BlockSpec(memory_space=pltpu.SMEM)
     attended, base = pl.pallas_call(
         functools.partial(fused_kernel, (n_seq, n_uly, group)),
         out_shape=(pltpu.VMEM((tokens, features), bf16), pltpu.VMEM((tokens, features), f32)),
-        in_specs=[scalars, scalars, anywhere, anywhere, anywhere, anywhere],
+        in_specs=[anywhere] * 6,
         out_specs=[pl.BlockSpec(memory_space=pltpu.VMEM)] * 2,
         scratch_shapes=[
+            pltpu.SMEM(dwa_slot.shape, jnp.int32),
+            pltpu.SMEM(dwa_table.shape, f32),
             pltpu.VMEM((3, tokens, features), bf16),
             pltpu.VMEM((stored, tokens, features), bf16),
             pltpu.VMEM((3, group, n_seq, rows, HEAD_DIM), bf16),
@@ -574,9 +574,10 @@
             pltpu.VMEM((2, n_uly, tokens + STAT, HEAD_DIM), bf16),
             pltpu.SemaphoreType.DMA,
             pltpu.SemaphoreType.DMA,
+            pltpu.SemaphoreType.DMA((2,)),
             pltpu.SemaphoreType.DMA,
             pltpu.SemaphoreType.DMA((2, n_uly)),
-            pltpu.SemaphoreType.DMA((n_uly,)),
+            pltpu.SemaphoreType.DMA((2, n_uly)),
             pltpu.SemaphoreType.DMA((3, group)),
             pltpu.SemaphoreType.DMA((3,)),
             pltpu.SemaphoreType.DMA,

time: 41 us -> 38.6 us (0.941)
  the two profiles are of different devices: /device:TPU:16 before, /device:TPU:24 now
where the time goes in v4:
time: 38.6 us; the launch traced here: 38.4 us
  Pallas kernels  37.5 us (97%)
  other arithmetic  0.9 us (2%)
    pallas_call x1, Pallas kernels, fused(): pl.pallas_call(functools.partial(fused_kernel, (n_seq, n_uly, group)), ou...  37.5 us
    convert_element_type x1, other arithmetic, fused(): return (base + attended.astype(f32)).astype(bf16)  0.9 us

profile of v4, /device:TPU:24, one launch (start us, length us, event | category | flops | bytes accessed | tf_op | source)
XLA Modules:
  0.0 38.4 jit_solution(2056862302514113445)
XLA Ops:
  0.0 37.5 %shard_map.64 = (bf16[128,2048]{1,0:T(8,128)(2,1)S(1)}, f32[128,2048]{1,0:T(8,128)S(1)}) custom-call(s32[2]{0:T(128)} %slot_hbm.1, f32[2,64]{1,0:T(2,128)} %table_hbm.1, bf16[128,2048]{1,0:T(8,128)(2,1)} %q_hbm.1, bf16[128,2048]{1,0:T(8,128)(2,1)} %k_hbm.1, bf16[128,2048]{1,0:T(8,128)(2,1)} %v_hbm.1, bf16[2,128,2048]{2,1,0:T(8,128)(2,1)} %past_hbm.1), custom_call_target="tpu_custom_call" | custom-call | tf_op jit(solution)/shard_map/pallas_call | solution.py:557
  37.5 0.9 %add_convert_fusion = bf16[128,2048]{1,0:T(8,128)(2,1)} fusion(f32[128,2048]{1,0:T(8,128)S(1)} %get-tuple-element.7, bf16[128,2048]{1,0:T(8,128)(2,1)S(1)} %get-tuple-element.8), kind=kLoop, calls=%fused_computation | loop fusion | flops 786432 | bytes 2097152 | tf_op jit(solution)/shard_map/convert_element_type | solution.py:597

commit v5 on v4

--- a/solution.py
+++ b/solution.py
@@ -104,11 +104,13 @@
     scale = math.log2(math.e) / HEAD_DIM**0.5
     s, t = lax.axis_index("seq"), lax.axis_index("uly")
     y, x = t // 2, t % 2
+    ahead = lax.axis_index("rep") % 2 == 1
+    behind = jnp.logical_not(ahead)
     peers = (t, 2 * y + 1 - x, 2 * (1 - y) + x, 3 - t)
     guests = range(max(1, group // 2))
     hosts = range(len(guests), group)
-    visit = group
-    lanes = {(Q, 2): 0, (Q, 3): 1, (K, 0): 2, (V, 0): 3, (K, 2): 2, (V, 2): 3, (K, 3): 2, (V, 3): 3}
+    visit = group - 1
+    lanes = {(Q, 2): 0, (Q, 3): 1, (K, 0): 2, (V, 0): 2, (K, 2): 2, (V, 2): 2, (K, 3): 2, (V, 3): 2}
 
     loads = [
         pltpu.make_async_copy(src, given.at[i], load_sem) for i, src in enumerate((q_hbm, k_hbm, v_hbm))
@@ -164,7 +166,8 @@
         landed(heads.at[kind, g, s, row_range(peers[d]), :], piece_sem.at[pieces, d])
 
     def arrived(kind, g, block):
-        landed(heads.at[kind, g, block], line_recv.at[lanes[kind, block], g])
+        ref = heads.at[Q, g, block] if kind == Q else heads.at[K:V + 1, g, block]
+        landed(ref, line_recv.at[lanes[kind, block], g])
 
     def pass_on(kind, g, d, block, to):
         dst = heads.at[kind, g, block, row_range(peers[d]), :]
@@ -311,17 +314,19 @@
 
     def join_last():
         landed(last_in.at[0], last_own)
-        for d in range(n_uly):
-            u = peers[d]
-            landed(last_in.at[1, u], last_far.at[u])
-            mine = level_of(last_in[0, u, tokens:tokens + STAT, :], 0)
-            theirs = level_of(last_in[1, u, tokens:tokens + STAT, :], 0)
-            top = jnp.maximum(mine, theirs)
-            mine, theirs = jnp.exp2(mine - top), jnp.exp2(theirs - top)
-            first = last_in[0, u, 0:tokens, :].astype(jnp.float32)
-            second = last_in[1, u, 0:tokens, :].astype(jnp.float32)
-            both = (first * mine + second * theirs) / (mine + theirs)
-            back[:, columns(u, group - 1)] = both.astype(jnp.bfloat16)
+        for pair in ((2, 3), (1, 0)):
+            for d in pair:
+                landed(last_in.at[1, peers[d]], last_far.at[peers[d]])
+            for d in pair:
+                u = peers[d]
+                mine = level_of(last_in[0, u, tokens:tokens + STAT, :], 0)
+                theirs = level_of(last_in[1, u, tokens:tokens + STAT, :], 0)
+                top = jnp.maximum(mine, theirs)
+                mine, theirs = jnp.exp2(mine - top), jnp.exp2(theirs - top)
+                first = last_in[0, u, 0:tokens, :].astype(jnp.float32)
+                second = last_in[1, u, 0:tokens, :].astype(jnp.float32)
+                both = (first * mine + second * theirs) / (mine + theirs)
+                back[:, columns(u, group - 1)] = both.astype(jnp.bfloat16)
         landed(back.at[:, 0:(group - 1) * n_uly * HEAD_DIM], back_sem)
 
     def merge(g, slot, a, lane=0):
@@ -377,15 +382,24 @@
 
     @pl.when(s == 0)
     def _():
-        for kind in (K, V):
-            pass_on(kind, 0, 0, 0, 1)
         order = [(kind, g) for g in range(group) for kind in (K, V)]
+        for kind, g in order[:2]:
+            pass_on(kind, g, 0, 0, 1)
+
+        @pl.when(ahead)
+        def _():
+            for kind, g in order[2:4]:
+                pass_on(kind, g, 0, 0, 1)
         for i, (kind, g) in enumerate(order):
             scatter(kind, g, i if g == 0 else None)
         for g in range(group):
             scatter(Q, g)
         for i, (kind, g) in enumerate(order):
-            if i + 2 < len(order):
+            if i < 2:
+                @pl.when(behind)
+                def _(i=i):
+                    pass_on(*order[i + 2], 0, 0, 1)
+            elif i + 2 < len(order):
                 pass_on(*order[i + 2], 0, 0, 1)
             forward(kind, g, 0, 1, i if g == 0 else None)
         for i in range(2):
@@ -410,16 +424,15 @@
                 scatter(kind, g)
         add_up()
 
-        def far(g, block, finish):
-            if block == 2:
-                for kind in (K, V):
-                    gathered(kind, g)
+        def begin(g, block):
             arrived(Q, g, block)
             attend(g, block, (1,), False, keep(block - 2))
-            if block == 2:
-                for kind in (K, V):
-                    arrived(kind, g, 0)
+
+        def end(g, block, finish):
             attend(g, block, (0,), False, finish, block - 2)
+
+        def earliest(g):
+            arrived(K, g, 0)
 
         def near(g):
             gathered(Q, g)
@@ -427,18 +440,29 @@
             give_back(g, (3, 2, 1, 0))
 
         def work(g):
-            far(g, 2, hand_over(g, 0))
+            for kind in (K, V):
+                gathered(kind, g)
+            begin(g, 2)
+            earliest(g)
+            end(g, 2, hand_over(g, 0))
             for a in (1 - y, y):
                 partial(g, 0, a, 2, g)
-            far(g, 3, hand_over(g, 1))
+            begin(g, 3)
+            end(g, 3, hand_over(g, 1))
             stays = g < len(guests)
             for a in (1 - y, y):
                 partial(g, 1, a, jnp.where(stays, 2, 3), jnp.where(stays, visit + g, g))
             near(g)
         each(0, group - 1, work)
-        for block in (2, 3):
-            far(group - 1, block, hand_out(block - 2))
-            send_last(block - 2, True, block)
+        for kind in (K, V):
+            gathered(kind, group - 1)
+        begin(group - 1, 3)
+        earliest(group - 1)
+        end(group - 1, 3, hand_out(1))
+        send_last(1, True, 3)
+        begin(group - 1, 2)
+        end(group - 1, 2, hand_out(0))
+        send_last(0, True, 2)
         near(group - 1)
         plane_sent()
         landed(part_out, part_send)
@@ -451,6 +475,11 @@
         pass_on(Q, 0, 0, 2, 1)
         for kind in (K, V):
             pass_on(kind, hosts[0], 0, 2, 3)
+
+        @pl.when(ahead)
+        def _():
+            for g in range(1, group):
+                pass_on(Q, g, 0, 2, 1)
         order = [(Q, 0), (Q, 1)]
         for g in hosts:
             order += [(K, g), (V, g)] + ([(Q, g)] if g > 1 else [])
@@ -462,10 +491,16 @@
                 scatter(kind, g)
         for kind, g in order:
             to = 1 if kind == Q else 3
-            if (g > 0 if kind == Q else g > hosts[0]):
-                pass_on(kind, g, 0, 2, to)
+            if kind == Q and g > 0:
+                @pl.when(behind)
+                def _(g=g):
+                    pass_on(Q, g, 0, 2, 1)
+            elif kind != Q and g > hosts[0]:
+                pass_on(kind, g, 0, 2, 3)
+            if kind == Q and g == max(2, group - 1):
+                relay(g)
             forward(kind, g, 2, to, g if kind == Q and g < 2 else None)
-            if kind == Q:
+            if kind == Q and g < max(2, group - 1):
                 relay(g)
         for g in range(2):
             gathered_piece(Q, g, 0, g)
@@ -480,8 +515,7 @@
             near(g)
 
         def receive(g):
-            for kind in (K, V):
-                arrived(kind, g, 3)
+            arrived(K, g, 3)
             attend(g, 3, (2,), True, keep(visit + g))
 
         attend(group - 1, 2, (), True, hand_out(0))
@@ -496,6 +530,7 @@
             receive(g)
             join(g, visit + g, 1)
         each(hosts[0], group - 1, join)
+        join_last()
         plane_sent()
         line_sent(Q, 2)
         for kind in (K, V):
@@ -504,12 +539,16 @@
         landed(last_out.at[0, 0:n_uly - 1], last_send)
         landed(att.at[1, 0:len(guests)], att_send.at[1])
         att_sent(0, group - 1)
-        join_last()
 
     @pl.when(s == 3)
     def _():
         for g in range(2):
             pass_on(Q, g, 0, 3, 2)
+
+        @pl.when(ahead)
+        def _():
+            for g in range(2, group):
+                pass_on(Q, g, 0, 3, 2)
         for g in range(group):
             scatter(Q, g, g if g < 2 else None)
         for g in (*guests, *hosts):
@@ -517,7 +556,9 @@
                 scatter(kind, g)
         for g in range(group):
             if g > 1:
-                pass_on(Q, g, 0, 3, 2)
+                @pl.when(behind)
+                def _(g=g):
+                    pass_on(Q, g, 0, 3, 2)
             forward(Q, g, 3, 2, g if g < 2 else None)
         for g in guests:
             for kind in (K, V):
@@ -530,19 +571,19 @@
         def near(g, finish=None):
             for kind in (K, V):
                 gathered(kind, g)
-                arrived(kind, g, 2)
+            arrived(K, g, 2)
             attend(g, 3, (2,), True, keep(g) if finish is None else finish)
         each(hosts[0], group - 1, near)
         near(group - 1, hand_out(0))
         send_last(0, False)
         each(hosts[0], group - 1, join)
+        join_last()
         plane_sent()
         line_sent(Q, 3)
         for kind in (K, V):
             line_sent(kind, 3, 0, len(guests))
         landed(last_out.at[0, 0:n_uly - 1], last_send)
         att_sent(hosts[0], group - 1)
-        join_last()
 
 
 def fused(queries, keys, values, past_outputs, dwa_slot, dwa_table):
@@ -550,7 +591,7 @@
     tokens, features = queries.shape
     group = features // n_uly // HEAD_DIM
     rows = tokens * n_uly
-    slots = group + max(1, group // 2)
+    slots = group - 1 + max(1, group // 2)
     stored = past_outputs.shape[0]
     bf16, f32 = jnp.bfloat16, jnp.float32
     anywhere = pl.BlockSpec(memory_space=pltpu.HBM)
@@ -581,7 +622,7 @@
             pltpu.SemaphoreType.DMA((3, group)),
             pltpu.SemaphoreType.DMA((3,)),
             pltpu.SemaphoreType.DMA,
-            pltpu.SemaphoreType.DMA((4, group)),
+            pltpu.SemaphoreType.DMA((3, group)),
             pltpu.SemaphoreType.DMA,
             pltpu.SemaphoreType.DMA((slots, 2)),
             pltpu.SemaphoreType.DMA((2,)),

time: 38.6 us -> 38.1 us (0.987)
  the two profiles are of different devices: /device:TPU:24 before, /device:TPU:16 now
where the time goes in v5:
time: 38.1 us; the launch traced here: 37.9 us
  Pallas kernels  37 us (97%)
  other arithmetic  0.9 us (2%)
    pallas_call x1, Pallas kernels, fused(): pl.pallas_call(functools.partial(fused_kernel, (n_seq, n_uly, group)), ou...  37 us
    convert_element_type x1, other arithmetic, fused(): return (base + attended.astype(f32)).astype(bf16)  0.9 us

profile of v5, /device:TPU:16, one launch (start us, length us, event | category | flops | bytes accessed | tf_op | source)
XLA Modules:
  0.0 37.9 jit_solution(2853831251241308041)
XLA Ops:
  0.0 37.0 %shard_map.64 = (bf16[128,2048]{1,0:T(8,128)(2,1)S(1)}, f32[128,2048]{1,0:T(8,128)S(1)}) custom-call(s32[2]{0:T(128)} %slot_hbm.1, f32[2,64]{1,0:T(2,128)} %table_hbm.1, bf16[128,2048]{1,0:T(8,128)(2,1)} %q_hbm.1, bf16[128,2048]{1,0:T(8,128)(2,1)} %k_hbm.1, bf16[128,2048]{1,0:T(8,128)(2,1)} %v_hbm.1, bf16[2,128,2048]{2,1,0:T(8,128)(2,1)} %past_hbm.1), custom_call_target="tpu_custom_call" | custom-call | tf_op jit(solution)/shard_map/pallas_call | solution.py:598
  37.0 0.9 %add_convert_fusion = bf16[128,2048]{1,0:T(8,128)(2,1)} fusion(f32[128,2048]{1,0:T(8,128)S(1)} %get-tuple-element.7, bf16[128,2048]{1,0:T(8,128)(2,1)S(1)} %get-tuple-element.8), kind=kLoop, calls=%fused_computation | loop fusion | flops 786432 | bytes 2097152 | tf_op jit(solution)/shard_map/convert_element_type | solution.py:638

commit v6 on v5

--- a/solution.py
+++ b/solution.py
@@ -94,7 +94,7 @@
     shape,
     slot_hbm, table_hbm, q_hbm, k_hbm, v_hbm, past_hbm, back, base_ref,
     slot_ref, table_ref, given, past, heads, own, own_stat, part_out, part_in, att, last_out, last_in,
-    load_sem, past_sem, table_sem, plane_send, piece_sem, relay_sem, whole_sem, line_send, extra_send, line_recv,
+    load_sem, past_sem, table_sem, plane_send, piece_sem, relay_sem, whole_sem, line_send, extra_send, line_recv, early_recv,
     part_send, part_recv, att_send, back_sem, last_send, last_own, last_far,
 ):
     n_seq, n_uly, group = shape
@@ -173,7 +173,10 @@
         dst = heads.at[kind, g, block, row_range(peers[d]), :]
         src = given.at[kind, :, columns(t, g)] if d == 0 else dst
         piecewise = kind == Q and block == 3 and g < 2
-        sem = relay_sem.at[g, d] if piecewise else line_recv.at[lanes[kind, block], g]
+        if block == 1:
+            sem = early_recv.at[1]
+        else:
+            sem = relay_sem.at[g, d] if piecewise else line_recv.at[lanes[kind, block], g]
         pltpu.make_async_remote_copy(
             src, dst, line_send.at[kind], sem,
             device_id={"seq": to}, device_id_type=MESH,
@@ -244,9 +247,9 @@
             top = new_top
         finish(top, total, acc)
 
-    def settle(g):
+    def settle(g, lane=0):
         def finish(top, total, acc):
-            att[0, g] = (acc / total).astype(jnp.bfloat16)
+            att[lane, g] = (acc / total).astype(jnp.bfloat16)
         return finish
 
     def keep(slot):
@@ -419,9 +422,20 @@
 
     @pl.when(s == 1)
     def _():
-        for g in range(group):
+        for kind in (K, V):
+            pass_on(kind, 0, 0, 1, 2)
+        for i, kind in enumerate((K, V)):
+            scatter(kind, 0, i)
+        for kind in (K, V):
+            scatter(kind, 1)
+        scatter(Q, 1)
+        scatter(Q, 0)
+        for g in range(2, group):
             for kind in (K, V, Q):
                 scatter(kind, g)
+        for i, kind in enumerate((K, V)):
+            forward(kind, 0, 1, 2, i)
+            gathered_piece(kind, 0, 0, i)
         add_up()
 
         def begin(g, block):
@@ -453,7 +467,14 @@
             for a in (1 - y, y):
                 partial(g, 1, a, jnp.where(stays, 2, 3), jnp.where(stays, visit + g, g))
             near(g)
-        each(0, group - 1, work)
+        earliest(0)
+        for kind in (K, V):
+            ref = heads.at[kind, 0, 0]
+            pltpu.make_async_remote_copy(
+                ref, ref, line_send.at[kind], early_recv.at[0], device_id={"seq": 2}, device_id_type=MESH
+            ).start()
+        near(0)
+        each(1, group - 1, work)
         for kind in (K, V):
             gathered(kind, group - 1)
         begin(group - 1, 3)
@@ -465,33 +486,36 @@
         send_last(0, True, 2)
         near(group - 1)
         plane_sent()
-        landed(part_out, part_send)
+        landed(part_out.at[1:], part_send)
+        for kind in (K, V):
+            landed(heads.at[kind, 0, 0:2], line_send.at[kind])
         landed(last_out, last_send)
         att_sent()
         landed(back, back_sem)
 
     @pl.when(s == 2)
     def _():
-        pass_on(Q, 0, 0, 2, 1)
         for kind in (K, V):
             pass_on(kind, hosts[0], 0, 2, 3)
+        pass_on(Q, 1, 0, 2, 1)
 
         @pl.when(ahead)
         def _():
-            for g in range(1, group):
+            for g in range(2, group):
                 pass_on(Q, g, 0, 2, 1)
-        order = [(Q, 0), (Q, 1)]
+        order = [(Q, 1)]
         for g in hosts:
             order += [(K, g), (V, g)] + ([(Q, g)] if g > 1 else [])
         order += [(Q, g) for g in range(2, hosts[0])]
         for kind, g in order:
             scatter(kind, g, g if kind == Q and g < 2 else None)
+        scatter(Q, 0)
         for g in guests:
             for kind in (K, V):
                 scatter(kind, g)
         for kind, g in order:
             to = 1 if kind == Q else 3
-            if kind == Q and g > 0:
+            if kind == Q and g > 1:
                 @pl.when(behind)
                 def _(g=g):
                     pass_on(Q, g, 0, 2, 1)
@@ -502,8 +526,7 @@
             forward(kind, g, 2, to, g if kind == Q and g < 2 else None)
             if kind == Q and g < max(2, group - 1):
                 relay(g)
-        for g in range(2):
-            gathered_piece(Q, g, 0, g)
+        gathered_piece(Q, 1, 0, 1)
         add_up()
 
         def near(g):
@@ -512,58 +535,61 @@
         def own_guest(g):
             for kind in (K, V):
                 gathered(kind, g)
-            near(g)
-
-        def receive(g):
-            arrived(K, g, 3)
-            attend(g, 3, (2,), True, keep(visit + g))
 
         attend(group - 1, 2, (), True, hand_out(0))
         send_last(0, False)
         each(hosts[0], group - 1, near)
-        each(0, len(guests), own_guest)
-        receive(0)
-        join(0)
-        join(0, visit, 1)
+        gathered(Q, 0)
+        own_guest(0)
+        for i in (1, 0):
+            landed(heads.at[K:V + 1, 0, i], early_recv.at[i])
+        attend(0, 2, (0, 1), True, settle(0))
+        give_back(0, (3, 2, 1, 0))
+        for d in range(n_uly):
+            landed(heads.at[Q, 0, 3, row_range(peers[d]), :], relay_sem.at[0, d])
+        arrived(K, 0, 3)
+        attend(0, 3, (0, 1, 2), True, settle(0, 1))
+        give_back(0, (3, 2, 1, 0), 1)
         for g in guests[1:]:
+            own_guest(g)
+            near(g)
             join(g)
-            receive(g)
+            arrived(K, g, 3)
+            attend(g, 3, (2,), True, keep(visit + g))
             join(g, visit + g, 1)
         each(hosts[0], group - 1, join)
         join_last()
         plane_sent()
-        line_sent(Q, 2)
+        line_sent(Q, 2, 1)
         for kind in (K, V):
             line_sent(kind, 2, hosts[0])
-        landed(heads.at[Q, :, 3], extra_send)
+        landed(heads.at[Q, 1:, 3], extra_send)
         landed(last_out.at[0, 0:n_uly - 1], last_send)
         landed(att.at[1, 0:len(guests)], att_send.at[1])
         att_sent(0, group - 1)
 
     @pl.when(s == 3)
     def _():
-        for g in range(2):
-            pass_on(Q, g, 0, 3, 2)
+        order = [(Q, g) for g in (*range(1, group), 0)] + [(kind, g) for g in guests for kind in (K, V)]
+        pass_on(Q, 1, 0, 3, 2)
 
         @pl.when(ahead)
         def _():
             for g in range(2, group):
                 pass_on(Q, g, 0, 3, 2)
-        for g in range(group):
-            scatter(Q, g, g if g < 2 else None)
-        for g in (*guests, *hosts):
+        for kind, g in order:
+            scatter(kind, g, g if kind == Q and g < 2 else None)
+        for g in hosts:
             for kind in (K, V):
                 scatter(kind, g)
-        for g in range(group):
-            if g > 1:
+        for kind, g in order:
+            if kind != Q or g == 0:
+                pass_on(kind, g, 0, 3, 2)
+            elif g > 1:
                 @pl.when(behind)
                 def _(g=g):
                     pass_on(Q, g, 0, 3, 2)
-            forward(Q, g, 3, 2, g if g < 2 else None)
-        for g in guests:
-            for kind in (K, V):
-                pass_on(kind, g, 0, 3, 2)
-                forward(kind, g, 3, 2)
+            forward(kind, g, 3, 2, g if kind == Q and g < 2 else None)
         for g in range(2):
             gathered_piece(Q, g, 0, g)
         add_up()
@@ -623,6 +649,7 @@
             pltpu.SemaphoreType.DMA((3,)),
             pltpu.SemaphoreType.DMA,
             pltpu.SemaphoreType.DMA((3, group)),
+            pltpu.SemaphoreType.DMA((2,)),
             pltpu.SemaphoreType.DMA,
             pltpu.SemaphoreType.DMA((slots, 2)),
             pltpu.SemaphoreType.DMA((2,)),

time: 38.1 us -> 38 us (level)
  no operation moved by 1% of the time
where the time goes in v6:
time: 38 us; the launch traced here: 37.8 us
  Pallas kernels  36.9 us (97%)
  other arithmetic  0.9 us (2%)
    pallas_call x1, Pallas kernels, fused(): pl.pallas_call(functools.partial(fused_kernel, (n_seq, n_uly, group)), ou...  36.9 us
    convert_element_type x1, other arithmetic, fused(): return (base + attended.astype(f32)).astype(bf16)  0.9 us

profile of v6, /device:TPU:16, one launch (start us, length us, event | category | flops | bytes accessed | tf_op | source)
XLA Modules:
  0.0 37.8 jit_solution(15842971068339391724)
XLA Ops:
  0.0 36.9 %shard_map.64 = (bf16[128,2048]{1,0:T(8,128)(2,1)S(1)}, f32[128,2048]{1,0:T(8,128)S(1)}) custom-call(s32[2]{0:T(128)} %slot_hbm.1, f32[2,64]{1,0:T(2,128)} %table_hbm.1, bf16[128,2048]{1,0:T(8,128)(2,1)} %q_hbm.1, bf16[128,2048]{1,0:T(8,128)(2,1)} %k_hbm.1, bf16[128,2048]{1,0:T(8,128)(2,1)} %v_hbm.1, bf16[2,128,2048]{2,1,0:T(8,128)(2,1)} %past_hbm.1), custom_call_target="tpu_custom_call" | custom-call | tf_op jit(solution)/shard_map/pallas_call | solution.py:624
  36.9 0.9 %add_convert_fusion = bf16[128,2048]{1,0:T(8,128)(2,1)} fusion(f32[128,2048]{1,0:T(8,128)S(1)} %get-tuple-element.7, bf16[128,2048]{1,0:T(8,128)(2,1)S(1)} %get-tuple-element.8), kind=kLoop, calls=%fused_computation | loop fusion | flops 786432 | bytes 2097152 | tf_op jit(solution)/shard_map/convert_element_type | solution.py:665

commit v7 on v6

--- a/solution.py
+++ b/solution.py
@@ -109,7 +109,7 @@
     peers = (t, 2 * y + 1 - x, 2 * (1 - y) + x, 3 - t)
     guests = range(max(1, group // 2))
     hosts = range(len(guests), group)
-    visit = group - 1
+    visit = group - 2
     lanes = {(Q, 2): 0, (Q, 3): 1, (K, 0): 2, (V, 0): 2, (K, 2): 2, (V, 2): 2, (K, 3): 2, (V, 3): 2}
 
     loads = [
@@ -172,11 +172,11 @@
     def pass_on(kind, g, d, block, to):
         dst = heads.at[kind, g, block, row_range(peers[d]), :]
         src = given.at[kind, :, columns(t, g)] if d == 0 else dst
-        piecewise = kind == Q and block == 3 and g < 2
+        piecewise = kind == Q and block == 3 and g == 1
         if block == 1:
             sem = early_recv.at[1]
         else:
-            sem = relay_sem.at[g, d] if piecewise else line_recv.at[lanes[kind, block], g]
+            sem = relay_sem.at[d] if piecewise else line_recv.at[lanes[kind, block], g]
         pltpu.make_async_remote_copy(
             src, dst, line_send.at[kind], sem,
             device_id={"seq": to}, device_id_type=MESH,
@@ -192,10 +192,10 @@
 
     def relay(g):
         parts = [heads.at[Q, g, 3]]
-        if g < 2:
+        if g == 1:
             parts = [heads.at[Q, g, 3, row_range(peers[d]), :] for d in range(n_uly)]
         for d, ref in enumerate(parts):
-            landed(ref, relay_sem.at[g, d] if g < 2 else line_recv.at[lanes[Q, 3], g])
+            landed(ref, relay_sem.at[d] if g == 1 else line_recv.at[lanes[Q, 3], g])
             pltpu.make_async_remote_copy(
                 ref, ref, extra_send, line_recv.at[lanes[Q, 3], g], device_id={"seq": 1}, device_id_type=MESH
             ).start()
@@ -545,8 +545,7 @@
             landed(heads.at[K:V + 1, 0, i], early_recv.at[i])
         attend(0, 2, (0, 1), True, settle(0))
         give_back(0, (3, 2, 1, 0))
-        for d in range(n_uly):
-            landed(heads.at[Q, 0, 3, row_range(peers[d]), :], relay_sem.at[0, d])
+        arrived(Q, 0, 3)
         arrived(K, 0, 3)
         attend(0, 3, (0, 1, 2), True, settle(0, 1))
         give_back(0, (3, 2, 1, 0), 1)
@@ -617,7 +616,7 @@
     tokens, features = queries.shape
     group = features // n_uly // HEAD_DIM
     rows = tokens * n_uly
-    slots = group - 1 + max(1, group // 2)
+    slots = max(2, group - 2 + max(1, group // 2))
     stored = past_outputs.shape[0]
     bf16, f32 = jnp.bfloat16, jnp.float32
     anywhere = pl.BlockSpec(memory_space=pltpu.HBM)
@@ -644,7 +643,7 @@
             pltpu.SemaphoreType.DMA((2,)),
             pltpu.SemaphoreType.DMA,
             pltpu.SemaphoreType.DMA((2, n_uly)),
-            pltpu.SemaphoreType.DMA((2, n_uly)),
+            pltpu.SemaphoreType.DMA((n_uly,)),
             pltpu.SemaphoreType.DMA((3, group)),
             pltpu.SemaphoreType.DMA((3,)),
             pltpu.SemaphoreType.DMA,

time: 38 us -> 38 us (level)
  no operation moved by 1% of the time
where the time goes in v7:
time: 38 us; the launch traced here: 37.7 us
  Pallas kernels  36.8 us (97%)
  other arithmetic  0.9 us (2%)
    pallas_call x1, Pallas kernels, fused(): pl.pallas_call(functools.partial(fused_kernel, (n_seq, n_uly, group)), ou...  36.8 us
    convert_element_type x1, other arithmetic, fused(): return (base + attended.astype(f32)).astype(bf16)  0.9 us

profile of v7, /device:TPU:16, one launch (start us, length us, event | category | flops | bytes accessed | tf_op | source)
XLA Modules:
  0.0 37.7 jit_solution(14252418449522406976)
XLA Ops:
  0.0 36.8 %shard_map.64 = (bf16[128,2048]{1,0:T(8,128)(2,1)S(1)}, f32[128,2048]{1,0:T(8,128)S(1)}) custom-call(s32[2]{0:T(128)} %slot_hbm.1, f32[2,64]{1,0:T(2,128)} %table_hbm.1, bf16[128,2048]{1,0:T(8,128)(2,1)} %q_hbm.1, bf16[128,2048]{1,0:T(8,128)(2,1)} %k_hbm.1, bf16[128,2048]{1,0:T(8,128)(2,1)} %v_hbm.1, bf16[2,128,2048]{2,1,0:T(8,128)(2,1)} %past_hbm.1), custom_call_target="tpu_custom_call" | custom-call | tf_op jit(solution)/shard_map/pallas_call | solution.py:623
  36.8 0.9 %add_convert_fusion = bf16[128,2048]{1,0:T(8,128)(2,1)} fusion(f32[128,2048]{1,0:T(8,128)S(1)} %get-tuple-element.7, bf16[128,2048]{1,0:T(8,128)(2,1)S(1)} %get-tuple-element.8), kind=kLoop, calls=%fused_computation | loop fusion | flops 786432 | bytes 2097152 | tf_op jit(solution)/shard_map/convert_element_type | solution.py:664
